TPU v7x, 16 devices: a whole 2x2x2 slice. The times are simulated.
16 devices in a mesh: dp: 16 (over z, y, x, core).
Axes of the slice: x: 2, y: 2, z: 2, core: 2. Of those that a mesh axis runs over, the one named last changes fastest.
Arguments:
- img_emb: bfloat16 [16384, 1152], P('dp')
- txt_emb: bfloat16 [16384, 1152], P('dp')
- log_temp: float32 [], replicated
- logit_bias: float32 [], replicated
Outputs:
- output 1: float32 [], replicated
- output 2: float32 [16384, 1152], P('dp')
- output 3: float32 [16384, 1152], P('dp')
- output 4: float32 [], replicated
- output 5: float32 [], replicated
All inputs are finite; a program needn't handle non-finite values.
Results may differ from a plain program's by a relative error of at most 0.001.
Values are sent between devices in bfloat16 or wider.
A program may use at most 1 GiB of HBM per device.

v0:
```python
import jax
import jax.numpy as jnp
from jax import lax
from jax.sharding import PartitionSpec as P


def normalize_rows(emb):
    emb32 = emb.astype(jnp.float32)
    inv_norm = lax.rsqrt(jnp.sum(emb32 * emb32, axis=-1, keepdims=True))
    return emb32 * inv_norm, inv_norm


def project_back(unit_rows, inv_norm, grad_dir):
    radial = jnp.sum(unit_rows * grad_dir, axis=-1, keepdims=True)
    return (grad_dir - unit_rows * radial) * inv_norm


def pair_terms(img_b, txt_blk, temp_scale, logit_bias, label_signs):
    sim_vals = jnp.einsum('id,jd->ij', img_b, txt_blk, preferred_element_type=jnp.float32)
    logits = temp_scale * sim_vals + logit_bias
    weights = -label_signs * jax.nn.sigmoid(-label_signs * logits)
    weights_b = weights.astype(jnp.bfloat16)
    img_part = jnp.einsum('ij,jd->id', weights_b, txt_blk, preferred_element_type=jnp.float32)
    txt_part = jnp.einsum('ij,id->jd', weights_b, img_b, preferred_element_type=jnp.float32)
    stat_sums = jnp.stack([
        jnp.sum(jax.nn.softplus(-label_signs * logits)),
        jnp.sum(weights),
        jnp.sum(weights * sim_vals),
    ])
    return img_part, txt_part, stat_sums


def solution(mesh):
    group_size = mesh.shape['dp']
    shift_pairs = [(src_dev, (src_dev + 1) % group_size) for src_dev in range(group_size)]

    def local_fn(img_emb, txt_emb, log_temp, logit_bias):
        rows_dev = img_emb.shape[0]
        total_rows = rows_dev * group_size
        img_unit, img_inv = normalize_rows(img_emb)
        txt_unit, txt_inv = normalize_rows(txt_emb)
        img_b = img_unit.astype(jnp.bfloat16)
        txt_b = txt_unit.astype(jnp.bfloat16)
        temp_scale = jnp.exp(log_temp)
        local_ids = jnp.arange(rows_dev)
        diag_signs = jnp.where(local_ids[:, None] == local_ids[None, :], 1.0, -1.0)
        img_acc, txt_acc, stat_sums = pair_terms(img_b, txt_b, temp_scale, logit_bias, diag_signs)

        def visit_step(step_idx, loop_state):
            txt_blk, txt_acc, img_acc, stat_sums = loop_state
            txt_blk = lax.ppermute(txt_blk, 'dp', shift_pairs)
            txt_acc = lax.ppermute(txt_acc, 'dp', shift_pairs)
            img_part, txt_part, new_sums = pair_terms(img_b, txt_blk, temp_scale, logit_bias, -1.0)
            return txt_blk, txt_acc + txt_part, img_acc + img_part, stat_sums + new_sums

        loop_state = lax.fori_loop(0, group_size - 1, visit_step, (txt_b, txt_acc, img_acc, stat_sums))
        txt_acc = lax.ppermute(loop_state[1], 'dp', shift_pairs)
        img_acc = loop_state[2]
        stat_sums = lax.psum(loop_state[3], 'dp') / total_rows
        grad_img = project_back(img_unit, img_inv, temp_scale * img_acc)
        grad_txt = project_back(txt_unit, txt_inv, temp_scale * txt_acc)
        return stat_sums[0], grad_img, grad_txt, temp_scale * stat_sums[2], stat_sums[1]

    return jax.shard_map(
        local_fn,
        mesh=mesh,
        in_specs=(P('dp', None), P('dp', None), P(), P()),
        out_specs=(P(), P('dp', None), P('dp', None), P(), P()),
        check_vma=False,
    )
```

profile of v0, /device:TPU:0, one launch (start us, length us, event | category | flops | bytes accessed | tf_op | source)
XLA Modules:
  0.0 1440.5 jit_solution(9738933016394017984)
XLA Ops:
  28.9 1314.5 %while.16 = (s32[]{:T(128)}, bf16[1024,1152]{1,0:T(8,128)(2,1)}, f32[1024,1152]{1,0:T(8,128)}, f32[1024,1152]{1,0:T(8,128)}, f32[3]{0:T(128)S(1)}, /*index=5*/f3...) while((s32[]{:T(128)}, bf16[1024,1152]{1,0:T(8,128)(2,1)}, f32[1024,1152]{1,0:T(8,128)}, ...), condition=%wide.region_9.10_spmd, body=%wide.region_5.9_spmd.sunk | while | flops 7278428160 | bytes 116392288 | solution.py:56
  32.5 27.8 %collective-permute-done = bf16[1024,1152]{1,0:T(8,128)(2,1)S(1)} collective-permute-done((bf16[1024,1152]{1,0:T(8,128)(2,1)}, bf16[1024,1152]{1,0:T(8,128)(2,1)S(1)}, u32[]{:S(2)}, u32[]{:S(2)}) %collective-permute-start) | collective-permute-done | bytes 2359328 | tf_op jit(solution)/shard_map/while/body/eval_jaxpr/ppermute | solution.py:51
  75.5 35.3 %collective-permute-done.1 = f32[1024,1152]{1,0:T(8,128)} collective-permute-done((f32[1024,1152]{1,0:T(8,128)}, f32[1024,1152]{1,0:T(8,128)}, u32[]{:S(2)}, u32[]{:S(2)}) %collective-permute-start.1) | collective-permute-done | bytes 4718624 | tf_op jit(solution)/shard_map/while/body/eval_jaxpr/ppermute | solution.py:52
  118.2 29.6 %collective-permute-done = bf16[1024,1152]{1,0:T(8,128)(2,1)S(1)} collective-permute-done((bf16[1024,1152]{1,0:T(8,128)(2,1)}, bf16[1024,1152]{1,0:T(8,128)(2,1)S(1)}, u32[]{:S(2)}, u32[]{:S(2)}) %collective-permute-start) | collective-permute-done | bytes 2359328 | tf_op jit(solution)/shard_map/while/body/eval_jaxpr/ppermute | solution.py:51
  163.1 35.3 %collective-permute-done.1 = f32[1024,1152]{1,0:T(8,128)} collective-permute-done((f32[1024,1152]{1,0:T(8,128)}, f32[1024,1152]{1,0:T(8,128)}, u32[]{:S(2)}, u32[]{:S(2)}) %collective-permute-start.1) | collective-permute-done | bytes 4718624 | tf_op jit(solution)/shard_map/while/body/eval_jaxpr/ppermute | solution.py:52
  205.3 30.0 %collective-permute-done = bf16[1024,1152]{1,0:T(8,128)(2,1)S(1)} collective-permute-done((bf16[1024,1152]{1,0:T(8,128)(2,1)}, bf16[1024,1152]{1,0:T(8,128)(2,1)S(1)}, u32[]{:S(2)}, u32[]{:S(2)}) %collective-permute-start) | collective-permute-done | bytes 2359328 | tf_op jit(solution)/shard_map/while/body/eval_jaxpr/ppermute | solution.py:51
  250.7 35.3 %collective-permute-done.1 = f32[1024,1152]{1,0:T(8,128)} collective-permute-done((f32[1024,1152]{1,0:T(8,128)}, f32[1024,1152]{1,0:T(8,128)}, u32[]{:S(2)}, u32[]{:S(2)}) %collective-permute-start.1) | collective-permute-done | bytes 4718624 | tf_op jit(solution)/shard_map/while/body/eval_jaxpr/ppermute | solution.py:52
  292.9 30.0 %collective-permute-done = bf16[1024,1152]{1,0:T(8,128)(2,1)S(1)} collective-permute-done((bf16[1024,1152]{1,0:T(8,128)(2,1)}, bf16[1024,1152]{1,0:T(8,128)(2,1)S(1)}, u32[]{:S(2)}, u32[]{:S(2)}) %collective-permute-start) | collective-permute-done | bytes 2359328 | tf_op jit(solution)/shard_map/while/body/eval_jaxpr/ppermute | solution.py:51
  338.2 35.3 %collective-permute-done.1 = f32[1024,1152]{1,0:T(8,128)} collective-permute-done((f32[1024,1152]{1,0:T(8,128)}, f32[1024,1152]{1,0:T(8,128)}, u32[]{:S(2)}, u32[]{:S(2)}) %collective-permute-start.1) | collective-permute-done | bytes 4718624 | tf_op jit(solution)/shard_map/while/body/eval_jaxpr/ppermute | solution.py:52
  380.4 30.0 %collective-permute-done = bf16[1024,1152]{1,0:T(8,128)(2,1)S(1)} collective-permute-done((bf16[1024,1152]{1,0:T(8,128)(2,1)}, bf16[1024,1152]{1,0:T(8,128)(2,1)S(1)}, u32[]{:S(2)}, u32[]{:S(2)}) %collective-permute-start) | collective-permute-done | bytes 2359328 | tf_op jit(solution)/shard_map/while/body/eval_jaxpr/ppermute | solution.py:51
  425.7 35.3 %collective-permute-done.1 = f32[1024,1152]{1,0:T(8,128)} collective-permute-done((f32[1024,1152]{1,0:T(8,128)}, f32[1024,1152]{1,0:T(8,128)}, u32[]{:S(2)}, u32[]{:S(2)}) %collective-permute-start.1) | collective-permute-done | bytes 4718624 | tf_op jit(solution)/shard_map/while/body/eval_jaxpr/ppermute | solution.py:52
  468.0 30.0 %collective-permute-done = bf16[1024,1152]{1,0:T(8,128)(2,1)S(1)} collective-permute-done((bf16[1024,1152]{1,0:T(8,128)(2,1)}, bf16[1024,1152]{1,0:T(8,128)(2,1)S(1)}, u32[]{:S(2)}, u32[]{:S(2)}) %collective-permute-start) | collective-permute-done | bytes 2359328 | tf_op jit(solution)/shard_map/while/body/eval_jaxpr/ppermute | solution.py:51
  513.3 35.3 %collective-permute-done.1 = f32[1024,1152]{1,0:T(8,128)} collective-permute-done((f32[1024,1152]{1,0:T(8,128)}, f32[1024,1152]{1,0:T(8,128)}, u32[]{:S(2)}, u32[]{:S(2)}) %collective-permute-start.1) | collective-permute-done | bytes 4718624 | tf_op jit(solution)/shard_map/while/body/eval_jaxpr/ppermute | solution.py:52
  555.5 30.0 %collective-permute-done = bf16[1024,1152]{1,0:T(8,128)(2,1)S(1)} collective-permute-done((bf16[1024,1152]{1,0:T(8,128)(2,1)}, bf16[1024,1152]{1,0:T(8,128)(2,1)S(1)}, u32[]{:S(2)}, u32[]{:S(2)}) %collective-permute-start) | collective-permute-done | bytes 2359328 | tf_op jit(solution)/shard_map/while/body/eval_jaxpr/ppermute | solution.py:51
  600.8 35.3 %collective-permute-done.1 = f32[1024,1152]{1,0:T(8,128)} collective-permute-done((f32[1024,1152]{1,0:T(8,128)}, f32[1024,1152]{1,0:T(8,128)}, u32[]{:S(2)}, u32[]{:S(2)}) %collective-permute-start.1) | collective-permute-done | bytes 4718624 | tf_op jit(solution)/shard_map/while/body/eval_jaxpr/ppermute | solution.py:52
  643.1 30.0 %collective-permute-done = bf16[1024,1152]{1,0:T(8,128)(2,1)S(1)} collective-permute-done((bf16[1024,1152]{1,0:T(8,128)(2,1)}, bf16[1024,1152]{1,0:T(8,128)(2,1)S(1)}, u32[]{:S(2)}, u32[]{:S(2)}) %collective-permute-start) | collective-permute-done | bytes 2359328 | tf_op jit(solution)/shard_map/while/body/eval_jaxpr/ppermute | solution.py:51
  688.4 35.3 %collective-permute-done.1 = f32[1024,1152]{1,0:T(8,128)} collective-permute-done((f32[1024,1152]{1,0:T(8,128)}, f32[1024,1152]{1,0:T(8,128)}, u32[]{:S(2)}, u32[]{:S(2)}) %collective-permute-start.1) | collective-permute-done | bytes 4718624 | tf_op jit(solution)/shard_map/while/body/eval_jaxpr/ppermute | solution.py:52
  730.7 30.0 %collective-permute-done = bf16[1024,1152]{1,0:T(8,128)(2,1)S(1)} collective-permute-done((bf16[1024,1152]{1,0:T(8,128)(2,1)}, bf16[1024,1152]{1,0:T(8,128)(2,1)S(1)}, u32[]{:S(2)}, u32[]{:S(2)}) %collective-permute-start) | collective-permute-done | bytes 2359328 | tf_op jit(solution)/shard_map/while/body/eval_jaxpr/ppermute | solution.py:51
  776.0 35.3 %collective-permute-done.1 = f32[1024,1152]{1,0:T(8,128)} collective-permute-done((f32[1024,1152]{1,0:T(8,128)}, f32[1024,1152]{1,0:T(8,128)}, u32[]{:S(2)}, u32[]{:S(2)}) %collective-permute-start.1) | collective-permute-done | bytes 4718624 | tf_op jit(solution)/shard_map/while/body/eval_jaxpr/ppermute | solution.py:52
  818.2 30.0 %collective-permute-done = bf16[1024,1152]{1,0:T(8,128)(2,1)S(1)} collective-permute-done((bf16[1024,1152]{1,0:T(8,128)(2,1)}, bf16[1024,1152]{1,0:T(8,128)(2,1)S(1)}, u32[]{:S(2)}, u32[]{:S(2)}) %collective-permute-start) | collective-permute-done | bytes 2359328 | tf_op jit(solution)/shard_map/while/body/eval_jaxpr/ppermute | solution.py:51
  863.5 35.3 %collective-permute-done.1 = f32[1024,1152]{1,0:T(8,128)} collective-permute-done((f32[1024,1152]{1,0:T(8,128)}, f32[1024,1152]{1,0:T(8,128)}, u32[]{:S(2)}, u32[]{:S(2)}) %collective-permute-start.1) | collective-permute-done | bytes 4718624 | tf_op jit(solution)/shard_map/while/body/eval_jaxpr/ppermute | solution.py:52
  905.8 30.0 %collective-permute-done = bf16[1024,1152]{1,0:T(8,128)(2,1)S(1)} collective-permute-done((bf16[1024,1152]{1,0:T(8,128)(2,1)}, bf16[1024,1152]{1,0:T(8,128)(2,1)S(1)}, u32[]{:S(2)}, u32[]{:S(2)}) %collective-permute-start) | collective-permute-done | bytes 2359328 | tf_op jit(solution)/shard_map/while/body/eval_jaxpr/ppermute | solution.py:51
  951.0 35.3 %collective-permute-done.1 = f32[1024,1152]{1,0:T(8,128)} collective-permute-done((f32[1024,1152]{1,0:T(8,128)}, f32[1024,1152]{1,0:T(8,128)}, u32[]{:S(2)}, u32[]{:S(2)}) %collective-permute-start.1) | collective-permute-done | bytes 4718624 | tf_op jit(solution)/shard_map/while/body/eval_jaxpr/ppermute | solution.py:52
  993.3 30.0 %collective-permute-done = bf16[1024,1152]{1,0:T(8,128)(2,1)S(1)} collective-permute-done((bf16[1024,1152]{1,0:T(8,128)(2,1)}, bf16[1024,1152]{1,0:T(8,128)(2,1)S(1)}, u32[]{:S(2)}, u32[]{:S(2)}) %collective-permute-start) | collective-permute-done | bytes 2359328 | tf_op jit(solution)/shard_map/while/body/eval_jaxpr/ppermute | solution.py:51
  1038.6 35.3 %collective-permute-done.1 = f32[1024,1152]{1,0:T(8,128)} collective-permute-done((f32[1024,1152]{1,0:T(8,128)}, f32[1024,1152]{1,0:T(8,128)}, u32[]{:S(2)}, u32[]{:S(2)}) %collective-permute-start.1) | collective-permute-done | bytes 4718624 | tf_op jit(solution)/shard_map/while/body/eval_jaxpr/ppermute | solution.py:52
  1080.9 30.0 %collective-permute-done = bf16[1024,1152]{1,0:T(8,128)(2,1)S(1)} collective-permute-done((bf16[1024,1152]{1,0:T(8,128)(2,1)}, bf16[1024,1152]{1,0:T(8,128)(2,1)S(1)}, u32[]{:S(2)}, u32[]{:S(2)}) %collective-permute-start) | collective-permute-done | bytes 2359328 | tf_op jit(solution)/shard_map/while/body/eval_jaxpr/ppermute | solution.py:51
  1126.1 35.3 %collective-permute-done.1 = f32[1024,1152]{1,0:T(8,128)} collective-permute-done((f32[1024,1152]{1,0:T(8,128)}, f32[1024,1152]{1,0:T(8,128)}, u32[]{:S(2)}, u32[]{:S(2)}) %collective-permute-start.1) | collective-permute-done | bytes 4718624 | tf_op jit(solution)/shard_map/while/body/eval_jaxpr/ppermute | solution.py:52
  1168.4 30.0 %collective-permute-done = bf16[1024,1152]{1,0:T(8,128)(2,1)S(1)} collective-permute-done((bf16[1024,1152]{1,0:T(8,128)(2,1)}, bf16[1024,1152]{1,0:T(8,128)(2,1)S(1)}, u32[]{:S(2)}, u32[]{:S(2)}) %collective-permute-start) | collective-permute-done | bytes 2359328 | tf_op jit(solution)/shard_map/while/body/eval_jaxpr/ppermute | solution.py:51
  1213.7 35.3 %collective-permute-done.1 = f32[1024,1152]{1,0:T(8,128)} collective-permute-done((f32[1024,1152]{1,0:T(8,128)}, f32[1024,1152]{1,0:T(8,128)}, u32[]{:S(2)}, u32[]{:S(2)}) %collective-permute-start.1) | collective-permute-done | bytes 4718624 | tf_op jit(solution)/shard_map/while/body/eval_jaxpr/ppermute | solution.py:52
  1256.0 30.0 %collective-permute-done = bf16[1024,1152]{1,0:T(8,128)(2,1)S(1)} collective-permute-done((bf16[1024,1152]{1,0:T(8,128)(2,1)}, bf16[1024,1152]{1,0:T(8,128)(2,1)S(1)}, u32[]{:S(2)}, u32[]{:S(2)}) %collective-permute-start) | collective-permute-done | bytes 2359328 | tf_op jit(solution)/shard_map/while/body/eval_jaxpr/ppermute | solution.py:51
  1301.3 35.3 %collective-permute-done.1 = f32[1024,1152]{1,0:T(8,128)} collective-permute-done((f32[1024,1152]{1,0:T(8,128)}, f32[1024,1152]{1,0:T(8,128)}, u32[]{:S(2)}, u32[]{:S(2)}) %collective-permute-start.1) | collective-permute-done | bytes 4718624 | tf_op jit(solution)/shard_map/while/body/eval_jaxpr/ppermute | solution.py:52
  1343.5 78.1 %psum.7 = f32[3]{0:T(128)S(1)} all-reduce(f32[3]{0:T(128)S(1)} %get-tuple-element.49), channel_id=1, replica_groups=mesh['dp'=16] {'dp'}, use_global_device_ids=true, to_apply=%region_10.11 | all-reduce | flops 3 | bytes 24 | tf_op jit(solution)/shard_map/psum | solution.py:59
  (279 shorter events, 380.2 us)
Async XLA Ops:
  28.9 1393.9 %copy-start.12 = (f32[1024]{0:T(1024)S(1)}, f32[1024]{0:T(1024)}, u32[]{:S(2)}) copy-start(f32[1024]{0:T(1024)} %copy-done.11) | copy-start | bytes 12292
  29.1 31.2 %collective-permute-start = (bf16[1024,1152]{1,0:T(8,128)(2,1)}, bf16[1024,1152]{1,0:T(8,128)(2,1)S(1)}, u32[]{:S(2)}, u32[]{:S(2)}) collective-permute-start(bf16[1024,1152]{1,0:T(8,128)(2,1)} %get-tuple-element.148), channel_id=1, source_target_pairs={{0,1},{1,2},{2,3},{3,4},{4,5},{5,6},{6,7},{7,8},{8,9},{9,10},{10,1... | collective-permute-start | bytes 7077896 | tf_op jit(solution)/shard_map/while/body/eval_jaxpr/ppermute | solution.py:51
  29.9 81.0 %collective-permute-start.1 = (f32[1024,1152]{1,0:T(8,128)}, f32[1024,1152]{1,0:T(8,128)}, u32[]{:S(2)}, u32[]{:S(2)}) collective-permute-start(f32[1024,1152]{1,0:T(8,128)} %get-tuple-element.149), channel_id=1, source_target_pairs={{0,1},{1,2},{2,3},{3,4},{4,5},{5,6},{6,7},{7,8},{8,9},{9,10},{10,1... | collective-permute-start | bytes 14155784 | tf_op jit(solution)/shard_map/while/body/eval_jaxpr/ppermute | solution.py:52
  117.8 30.1 %collective-permute-start = (bf16[1024,1152]{1,0:T(8,128)(2,1)}, bf16[1024,1152]{1,0:T(8,128)(2,1)S(1)}, u32[]{:S(2)}, u32[]{:S(2)}) collective-permute-start(bf16[1024,1152]{1,0:T(8,128)(2,1)} %get-tuple-element.148), channel_id=1, source_target_pairs={{0,1},{1,2},{2,3},{3,4},{4,5},{5,6},{6,7},{7,8},{8,9},{9,10},{10,1... | collective-permute-start | bytes 7077896 | tf_op jit(solution)/shard_map/while/body/eval_jaxpr/ppermute | solution.py:51
  117.8 80.6 %collective-permute-start.1 = (f32[1024,1152]{1,0:T(8,128)}, f32[1024,1152]{1,0:T(8,128)}, u32[]{:S(2)}, u32[]{:S(2)}) collective-permute-start(f32[1024,1152]{1,0:T(8,128)} %get-tuple-element.149), channel_id=1, source_target_pairs={{0,1},{1,2},{2,3},{3,4},{4,5},{5,6},{6,7},{7,8},{8,9},{9,10},{10,1... | collective-permute-start | bytes 14155784 | tf_op jit(solution)/shard_map/while/body/eval_jaxpr/ppermute | solution.py:52
  205.3 30.1 %collective-permute-start = (bf16[1024,1152]{1,0:T(8,128)(2,1)}, bf16[1024,1152]{1,0:T(8,128)(2,1)S(1)}, u32[]{:S(2)}, u32[]{:S(2)}) collective-permute-start(bf16[1024,1152]{1,0:T(8,128)(2,1)} %get-tuple-element.148), channel_id=1, source_target_pairs={{0,1},{1,2},{2,3},{3,4},{4,5},{5,6},{6,7},{7,8},{8,9},{9,10},{10,1... | collective-permute-start | bytes 7077896 | tf_op jit(solution)/shard_map/while/body/eval_jaxpr/ppermute | solution.py:51
  205.3 80.6 %collective-permute-start.1 = (f32[1024,1152]{1,0:T(8,128)}, f32[1024,1152]{1,0:T(8,128)}, u32[]{:S(2)}, u32[]{:S(2)}) collective-permute-start(f32[1024,1152]{1,0:T(8,128)} %get-tuple-element.149), channel_id=1, source_target_pairs={{0,1},{1,2},{2,3},{3,4},{4,5},{5,6},{6,7},{7,8},{8,9},{9,10},{10,1... | collective-permute-start | bytes 14155784 | tf_op jit(solution)/shard_map/while/body/eval_jaxpr/ppermute | solution.py:52
  292.9 30.1 %collective-permute-start = (bf16[1024,1152]{1,0:T(8,128)(2,1)}, bf16[1024,1152]{1,0:T(8,128)(2,1)S(1)}, u32[]{:S(2)}, u32[]{:S(2)}) collective-permute-start(bf16[1024,1152]{1,0:T(8,128)(2,1)} %get-tuple-element.148), channel_id=1, source_target_pairs={{0,1},{1,2},{2,3},{3,4},{4,5},{5,6},{6,7},{7,8},{8,9},{9,10},{10,1... | collective-permute-start | bytes 7077896 | tf_op jit(solution)/shard_map/while/body/eval_jaxpr/ppermute | solution.py:51
  292.9 80.6 %collective-permute-start.1 = (f32[1024,1152]{1,0:T(8,128)}, f32[1024,1152]{1,0:T(8,128)}, u32[]{:S(2)}, u32[]{:S(2)}) collective-permute-start(f32[1024,1152]{1,0:T(8,128)} %get-tuple-element.149), channel_id=1, source_target_pairs={{0,1},{1,2},{2,3},{3,4},{4,5},{5,6},{6,7},{7,8},{8,9},{9,10},{10,1... | collective-permute-start | bytes 14155784 | tf_op jit(solution)/shard_map/while/body/eval_jaxpr/ppermute | solution.py:52
  380.4 30.1 %collective-permute-start = (bf16[1024,1152]{1,0:T(8,128)(2,1)}, bf16[1024,1152]{1,0:T(8,128)(2,1)S(1)}, u32[]{:S(2)}, u32[]{:S(2)}) collective-permute-start(bf16[1024,1152]{1,0:T(8,128)(2,1)} %get-tuple-element.148), channel_id=1, source_target_pairs={{0,1},{1,2},{2,3},{3,4},{4,5},{5,6},{6,7},{7,8},{8,9},{9,10},{10,1... | collective-permute-start | bytes 7077896 | tf_op jit(solution)/shard_map/while/body/eval_jaxpr/ppermute | solution.py:51
  380.4 80.6 %collective-permute-start.1 = (f32[1024,1152]{1,0:T(8,128)}, f32[1024,1152]{1,0:T(8,128)}, u32[]{:S(2)}, u32[]{:S(2)}) collective-permute-start(f32[1024,1152]{1,0:T(8,128)} %get-tuple-element.149), channel_id=1, source_target_pairs={{0,1},{1,2},{2,3},{3,4},{4,5},{5,6},{6,7},{7,8},{8,9},{9,10},{10,1... | collective-permute-start | bytes 14155784 | tf_op jit(solution)/shard_map/while/body/eval_jaxpr/ppermute | solution.py:52
  468.0 30.1 %collective-permute-start = (bf16[1024,1152]{1,0:T(8,128)(2,1)}, bf16[1024,1152]{1,0:T(8,128)(2,1)S(1)}, u32[]{:S(2)}, u32[]{:S(2)}) collective-permute-start(bf16[1024,1152]{1,0:T(8,128)(2,1)} %get-tuple-element.148), channel_id=1, source_target_pairs={{0,1},{1,2},{2,3},{3,4},{4,5},{5,6},{6,7},{7,8},{8,9},{9,10},{10,1... | collective-permute-start | bytes 7077896 | tf_op jit(solution)/shard_map/while/body/eval_jaxpr/ppermute | solution.py:51
  468.0 80.6 %collective-permute-start.1 = (f32[1024,1152]{1,0:T(8,128)}, f32[1024,1152]{1,0:T(8,128)}, u32[]{:S(2)}, u32[]{:S(2)}) collective-permute-start(f32[1024,1152]{1,0:T(8,128)} %get-tuple-element.149), channel_id=1, source_target_pairs={{0,1},{1,2},{2,3},{3,4},{4,5},{5,6},{6,7},{7,8},{8,9},{9,10},{10,1... | collective-permute-start | bytes 14155784 | tf_op jit(solution)/shard_map/while/body/eval_jaxpr/ppermute | solution.py:52
  555.5 30.1 %collective-permute-start = (bf16[1024,1152]{1,0:T(8,128)(2,1)}, bf16[1024,1152]{1,0:T(8,128)(2,1)S(1)}, u32[]{:S(2)}, u32[]{:S(2)}) collective-permute-start(bf16[1024,1152]{1,0:T(8,128)(2,1)} %get-tuple-element.148), channel_id=1, source_target_pairs={{0,1},{1,2},{2,3},{3,4},{4,5},{5,6},{6,7},{7,8},{8,9},{9,10},{10,1... | collective-permute-start | bytes 7077896 | tf_op jit(solution)/shard_map/while/body/eval_jaxpr/ppermute | solution.py:51
  555.5 80.6 %collective-permute-start.1 = (f32[1024,1152]{1,0:T(8,128)}, f32[1024,1152]{1,0:T(8,128)}, u32[]{:S(2)}, u32[]{:S(2)}) collective-permute-start(f32[1024,1152]{1,0:T(8,128)} %get-tuple-element.149), channel_id=1, source_target_pairs={{0,1},{1,2},{2,3},{3,4},{4,5},{5,6},{6,7},{7,8},{8,9},{9,10},{10,1... | collective-permute-start | bytes 14155784 | tf_op jit(solution)/shard_map/while/body/eval_jaxpr/ppermute | solution.py:52
  643.1 30.1 %collective-permute-start = (bf16[1024,1152]{1,0:T(8,128)(2,1)}, bf16[1024,1152]{1,0:T(8,128)(2,1)S(1)}, u32[]{:S(2)}, u32[]{:S(2)}) collective-permute-start(bf16[1024,1152]{1,0:T(8,128)(2,1)} %get-tuple-element.148), channel_id=1, source_target_pairs={{0,1},{1,2},{2,3},{3,4},{4,5},{5,6},{6,7},{7,8},{8,9},{9,10},{10,1... | collective-permute-start | bytes 7077896 | tf_op jit(solution)/shard_map/while/body/eval_jaxpr/ppermute | solution.py:51
  643.1 80.6 %collective-permute-start.1 = (f32[1024,1152]{1,0:T(8,128)}, f32[1024,1152]{1,0:T(8,128)}, u32[]{:S(2)}, u32[]{:S(2)}) collective-permute-start(f32[1024,1152]{1,0:T(8,128)} %get-tuple-element.149), channel_id=1, source_target_pairs={{0,1},{1,2},{2,3},{3,4},{4,5},{5,6},{6,7},{7,8},{8,9},{9,10},{10,1... | collective-permute-start | bytes 14155784 | tf_op jit(solution)/shard_map/while/body/eval_jaxpr/ppermute | solution.py:52
  730.6 30.1 %collective-permute-start = (bf16[1024,1152]{1,0:T(8,128)(2,1)}, bf16[1024,1152]{1,0:T(8,128)(2,1)S(1)}, u32[]{:S(2)}, u32[]{:S(2)}) collective-permute-start(bf16[1024,1152]{1,0:T(8,128)(2,1)} %get-tuple-element.148), channel_id=1, source_target_pairs={{0,1},{1,2},{2,3},{3,4},{4,5},{5,6},{6,7},{7,8},{8,9},{9,10},{10,1... | collective-permute-start | bytes 7077896 | tf_op jit(solution)/shard_map/while/body/eval_jaxpr/ppermute | solution.py:51
  730.6 80.6 %collective-permute-start.1 = (f32[1024,1152]{1,0:T(8,128)}, f32[1024,1152]{1,0:T(8,128)}, u32[]{:S(2)}, u32[]{:S(2)}) collective-permute-start(f32[1024,1152]{1,0:T(8,128)} %get-tuple-element.149), channel_id=1, source_target_pairs={{0,1},{1,2},{2,3},{3,4},{4,5},{5,6},{6,7},{7,8},{8,9},{9,10},{10,1... | collective-permute-start | bytes 14155784 | tf_op jit(solution)/shard_map/while/body/eval_jaxpr/ppermute | solution.py:52
  818.2 30.1 %collective-permute-start = (bf16[1024,1152]{1,0:T(8,128)(2,1)}, bf16[1024,1152]{1,0:T(8,128)(2,1)S(1)}, u32[]{:S(2)}, u32[]{:S(2)}) collective-permute-start(bf16[1024,1152]{1,0:T(8,128)(2,1)} %get-tuple-element.148), channel_id=1, source_target_pairs={{0,1},{1,2},{2,3},{3,4},{4,5},{5,6},{6,7},{7,8},{8,9},{9,10},{10,1... | collective-permute-start | bytes 7077896 | tf_op jit(solution)/shard_map/while/body/eval_jaxpr/ppermute | solution.py:51
  818.2 80.6 %collective-permute-start.1 = (f32[1024,1152]{1,0:T(8,128)}, f32[1024,1152]{1,0:T(8,128)}, u32[]{:S(2)}, u32[]{:S(2)}) collective-permute-start(f32[1024,1152]{1,0:T(8,128)} %get-tuple-element.149), channel_id=1, source_target_pairs={{0,1},{1,2},{2,3},{3,4},{4,5},{5,6},{6,7},{7,8},{8,9},{9,10},{10,1... | collective-permute-start | bytes 14155784 | tf_op jit(solution)/shard_map/while/body/eval_jaxpr/ppermute | solution.py:52
  905.7 30.1 %collective-permute-start = (bf16[1024,1152]{1,0:T(8,128)(2,1)}, bf16[1024,1152]{1,0:T(8,128)(2,1)S(1)}, u32[]{:S(2)}, u32[]{:S(2)}) collective-permute-start(bf16[1024,1152]{1,0:T(8,128)(2,1)} %get-tuple-element.148), channel_id=1, source_target_pairs={{0,1},{1,2},{2,3},{3,4},{4,5},{5,6},{6,7},{7,8},{8,9},{9,10},{10,1... | collective-permute-start | bytes 7077896 | tf_op jit(solution)/shard_map/while/body/eval_jaxpr/ppermute | solution.py:51
  905.7 80.6 %collective-permute-start.1 = (f32[1024,1152]{1,0:T(8,128)}, f32[1024,1152]{1,0:T(8,128)}, u32[]{:S(2)}, u32[]{:S(2)}) collective-permute-start(f32[1024,1152]{1,0:T(8,128)} %get-tuple-element.149), channel_id=1, source_target_pairs={{0,1},{1,2},{2,3},{3,4},{4,5},{5,6},{6,7},{7,8},{8,9},{9,10},{10,1... | collective-permute-start | bytes 14155784 | tf_op jit(solution)/shard_map/while/body/eval_jaxpr/ppermute | solution.py:52
  993.3 30.1 %collective-permute-start = (bf16[1024,1152]{1,0:T(8,128)(2,1)}, bf16[1024,1152]{1,0:T(8,128)(2,1)S(1)}, u32[]{:S(2)}, u32[]{:S(2)}) collective-permute-start(bf16[1024,1152]{1,0:T(8,128)(2,1)} %get-tuple-element.148), channel_id=1, source_target_pairs={{0,1},{1,2},{2,3},{3,4},{4,5},{5,6},{6,7},{7,8},{8,9},{9,10},{10,1... | collective-permute-start | bytes 7077896 | tf_op jit(solution)/shard_map/while/body/eval_jaxpr/ppermute | solution.py:51
  993.3 80.6 %collective-permute-start.1 = (f32[1024,1152]{1,0:T(8,128)}, f32[1024,1152]{1,0:T(8,128)}, u32[]{:S(2)}, u32[]{:S(2)}) collective-permute-start(f32[1024,1152]{1,0:T(8,128)} %get-tuple-element.149), channel_id=1, source_target_pairs={{0,1},{1,2},{2,3},{3,4},{4,5},{5,6},{6,7},{7,8},{8,9},{9,10},{10,1... | collective-permute-start | bytes 14155784 | tf_op jit(solution)/shard_map/while/body/eval_jaxpr/ppermute | solution.py:52
  1080.8 30.1 %collective-permute-start = (bf16[1024,1152]{1,0:T(8,128)(2,1)}, bf16[1024,1152]{1,0:T(8,128)(2,1)S(1)}, u32[]{:S(2)}, u32[]{:S(2)}) collective-permute-start(bf16[1024,1152]{1,0:T(8,128)(2,1)} %get-tuple-element.148), channel_id=1, source_target_pairs={{0,1},{1,2},{2,3},{3,4},{4,5},{5,6},{6,7},{7,8},{8,9},{9,10},{10,1... | collective-permute-start | bytes 7077896 | tf_op jit(solution)/shard_map/while/body/eval_jaxpr/ppermute | solution.py:51
  1080.8 80.6 %collective-permute-start.1 = (f32[1024,1152]{1,0:T(8,128)}, f32[1024,1152]{1,0:T(8,128)}, u32[]{:S(2)}, u32[]{:S(2)}) collective-permute-start(f32[1024,1152]{1,0:T(8,128)} %get-tuple-element.149), channel_id=1, source_target_pairs={{0,1},{1,2},{2,3},{3,4},{4,5},{5,6},{6,7},{7,8},{8,9},{9,10},{10,1... | collective-permute-start | bytes 14155784 | tf_op jit(solution)/shard_map/while/body/eval_jaxpr/ppermute | solution.py:52
  1168.4 30.1 %collective-permute-start = (bf16[1024,1152]{1,0:T(8,128)(2,1)}, bf16[1024,1152]{1,0:T(8,128)(2,1)S(1)}, u32[]{:S(2)}, u32[]{:S(2)}) collective-permute-start(bf16[1024,1152]{1,0:T(8,128)(2,1)} %get-tuple-element.148), channel_id=1, source_target_pairs={{0,1},{1,2},{2,3},{3,4},{4,5},{5,6},{6,7},{7,8},{8,9},{9,10},{10,1... | collective-permute-start | bytes 7077896 | tf_op jit(solution)/shard_map/while/body/eval_jaxpr/ppermute | solution.py:51
  1168.4 80.6 %collective-permute-start.1 = (f32[1024,1152]{1,0:T(8,128)}, f32[1024,1152]{1,0:T(8,128)}, u32[]{:S(2)}, u32[]{:S(2)}) collective-permute-start(f32[1024,1152]{1,0:T(8,128)} %get-tuple-element.149), channel_id=1, source_target_pairs={{0,1},{1,2},{2,3},{3,4},{4,5},{5,6},{6,7},{7,8},{8,9},{9,10},{10,1... | collective-permute-start | bytes 14155784 | tf_op jit(solution)/shard_map/while/body/eval_jaxpr/ppermute | solution.py:52
  1255.9 30.1 %collective-permute-start = (bf16[1024,1152]{1,0:T(8,128)(2,1)}, bf16[1024,1152]{1,0:T(8,128)(2,1)S(1)}, u32[]{:S(2)}, u32[]{:S(2)}) collective-permute-start(bf16[1024,1152]{1,0:T(8,128)(2,1)} %get-tuple-element.148), channel_id=1, source_target_pairs={{0,1},{1,2},{2,3},{3,4},{4,5},{5,6},{6,7},{7,8},{8,9},{9,10},{10,1... | collective-permute-start | bytes 7077896 | tf_op jit(solution)/shard_map/while/body/eval_jaxpr/ppermute | solution.py:51
  1255.9 80.6 %collective-permute-start.1 = (f32[1024,1152]{1,0:T(8,128)}, f32[1024,1152]{1,0:T(8,128)}, u32[]{:S(2)}, u32[]{:S(2)}) collective-permute-start(f32[1024,1152]{1,0:T(8,128)} %get-tuple-element.149), channel_id=1, source_target_pairs={{0,1},{1,2},{2,3},{3,4},{4,5},{5,6},{6,7},{7,8},{8,9},{9,10},{10,1... | collective-permute-start | bytes 14155784 | tf_op jit(solution)/shard_map/while/body/eval_jaxpr/ppermute | solution.py:52
  1343.5 87.0 %collective-permute-start.2 = (f32[1024,1152]{1,0:T(8,128)}, f32[1024,1152]{1,0:T(8,128)}, u32[]{:S(2)}, u32[]{:S(2)}) collective-permute-start(f32[1024,1152]{1,0:T(8,128)} %get-tuple-element.51), channel_id=1, source_target_pairs={{0,1},{1,2},{2,3},{3,4},{4,5},{5,6},{6,7},{7,8},{8,9},{9,10},{10,1... | collective-permute-start | bytes 14155784 | tf_op jit(solution)/shard_map/ppermute | solution.py:57
  (70 other events, 1555.1 us)
where the time goes:
time: 1440 us
  waiting for transfers between devices  977 us (68%)
  matrix products  299 us (21%)
  blocking collectives  78.1 us (5%)
  other arithmetic  54.5 us (4%)
  local copies, waits for them, and re-layouts  23.1 us (2%)
    ppermute x15, waiting for transfers between devices, visit_step(): txt_acc = lax.ppermute(txt_acc, 'dp', shift_pairs)  530 us
    ppermute x15, waiting for transfers between devices, visit_step(): txt_blk = lax.ppermute(txt_blk, 'dp', shift_pairs)  448 us
    dot_general x16, matrix products, pair_terms(): jnp.einsum('id,jd->ij', img_b, txt_blk, preferred_element_type=jnp.float32)  126 us
    dot_general x16, matrix products, pair_terms(): jnp.einsum('ij,id->jd', weights_b, img_b, preferred_element_type=jnp.floa...  109 us
    psum x1, blocking collectives, local_fn(): stat_sums = lax.psum(loop_state[3], 'dp') / total_rows  78.1 us
    dot_general x16, matrix products, pair_terms(): jnp.einsum('ij,jd->id', weights_b, txt_blk, preferred_element_type=jnp.fl...  63.2 us
    add x15, other arithmetic, visit_step(): stat_sums + new_sums  30.7 us
  transfers between devices with their start and end apart: 31, of which 30 were waited for; matrix products, arithmetic and copies ran while one was open for 16% of the time, Pallas kernels for 0%

commit v1 on v0

v1 whole, which is shorter than its diff:
```python
import functools

import jax
import jax.numpy as jnp
from jax import lax
from jax.experimental import pallas as pl
from jax.experimental.pallas import tpu as pltpu
from jax.sharding import PartitionSpec as P

LOG2E = 1.4426950408889634
LN2 = 0.6931471805599453
MESH = pl.DeviceIdType.MESH
ROWS = 1024
WIDTH = 1152
PIECE = 512
HALVES = ROWS // PIECE
THIRD = WIDTH // 3
CORE, AX, AY, AZ = 1, 2, 4, 8
AXES = (AX, AY, AZ)

ORDER = (
    [(1, 0), (1, 1)]
    + [(m, 0) for m in (2, 4, 8, 3, 5, 9)]
    + [(m, 1) for m in (2, 4, 8, 3, 5, 9)]
    + [(m, 0) for m in (6, 12, 10, 7, 13, 11)]
    + [(m, 1) for m in (6, 12, 10, 7, 13, 11)]
    + [(14, 0), (15, 0), (14, 1), (15, 1)]
)
FORWARD = {
    2: [(AY, 384, 768, 0), (AZ, 384, 384, 0)],
    4: [(AZ, 0, 768, 0), (AX, 0, 384, 1)],
    8: [(AX, 0, 384, 1), (AX, 768, 384, 2), (AY, 768, 384, 1)],
    6: [(AZ, 384, 384, 0)],
    12: [(AX, 0, 384, 1)],
    10: [(AY, 768, 384, 2)],
}
PARTS = {1: [(0, WIDTH, 0)], 2: [(0, WIDTH, 0)], 4: [(0, WIDTH, 0)], 8: [(0, WIDTH, 0)]}
for _m, _sends in FORWARD.items():
    for _axis, _c0, _nc, _part in _sends:
        PARTS.setdefault(_m ^ _axis, []).append((_c0, _nc, _part))
for _m in (3, 5, 9, 7, 13, 11, 15):
    PARTS[_m] = [(0, WIDTH, 0)]


def normalize_rows(emb):
    emb32 = emb.astype(jnp.float32)
    inv_norm = lax.rsqrt(jnp.sum(emb32 * emb32, axis=-1, keepdims=True))
    return emb32 * inv_norm, inv_norm


def project_back(unit_rows, inv_norm, grad_dir):
    radial = jnp.sum(unit_rows * grad_dir, axis=-1, keepdims=True)
    return (grad_dir - unit_rows * radial) * inv_norm


def dot_t(a, b):
    return lax.dot_general(a, b, (((1,), (1,)), ((), ())), preferred_element_type=jnp.float32)


def dot_n(a, b):
    return lax.dot_general(a, b, (((1,), (0,)), ((), ())), preferred_element_type=jnp.float32)


def fold8(v):
    rows, cols = v.shape
    return jnp.sum(v.reshape(rows // 8, 8, cols), axis=0)


def text_weights(s, t2, b2, stats, row_off=None):
    rows, cols = s.shape
    step = 64
    out = []
    acc = [None, None, None]
    prod = None
    for r in range(0, rows, step):
        sc = s[r : r + step]
        logit = sc * t2 + b2
        small = jnp.exp2(-jnp.abs(logit))
        recip = 1.0 / (1.0 + small)
        other = small * recip
        pos = logit >= 0
        h = jnp.where(pos, recip, other)
        over = jnp.maximum(logit, 0.0)
        if row_off is not None:
            ri = lax.broadcasted_iota(jnp.int32, sc.shape, 0) + r
            ci = lax.broadcasted_iota(jnp.int32, sc.shape, 1) + row_off
            own = ri == ci
            h = jnp.where(own, -jnp.where(pos, other, recip), h)
            over = jnp.where(own, over - logit, over)
        sums = [fold8(over), fold8(h), fold8(h * sc)]
        acc = [b if a is None else a + b for a, b in zip(acc, sums)]
        q = small
        while q.shape[0] > 8:
            n = q.shape[0] // 2
            q = q[:n] + q[n:] + q[:n] * q[n:]
        if prod is None:
            prod = q
        elif (r // step) % 8 == 0:
            stats[3] += jnp.log1p(prod)
            prod = q
        else:
            prod = prod + q + prod * q
        out.append(h.astype(jnp.bfloat16))
    stats[3] += jnp.log1p(prod)
    for i in range(3):
        stats[i] += acc[i]
    return jnp.concatenate(out, axis=0)


def image_weights(s, t2, b2, row_off=None):
    logit = s * t2 + b2
    if row_off is None:
        return (1.0 / (1.0 + jnp.exp2(-logit))).astype(jnp.bfloat16)
    ri = lax.broadcasted_iota(jnp.int32, s.shape, 0)
    ci = lax.broadcasted_iota(jnp.int32, s.shape, 1) + row_off
    own = ri == ci
    h = 1.0 / (1.0 + jnp.exp2(jnp.where(own, logit, -logit)))
    return jnp.where(own, -h, h).astype(jnp.bfloat16)


def kernel(par, xb, yb, au, av, stats, land, xo, yo, bufs, own_sem, buf_sem, send_sem, recv_sem):
    me = lax.axis_index("dp")

    def peer(axis):
        return me + axis * (1 - 2 * lax.rem(me // axis, 2))

    barrier = pltpu.get_barrier_semaphore()
    for axis in (CORE,) + AXES:
        pl.semaphore_signal(barrier, inc=1, device_id=(peer(axis),), device_id_type=MESH)

    own_copies = [
        pltpu.make_async_copy(xb, xo, own_sem.at[0]),
        pltpu.make_async_copy(yb, yo, own_sem.at[1]),
    ]
    for c in own_copies:
        c.start()
    au[...] = jnp.zeros_like(au)
    av[...] = jnp.zeros_like(av)
    stats[...] = jnp.zeros_like(stats)
    pl.semaphore_wait(barrier, 4)

    started = []
    mine = (xb, yb)

    def rows(half):
        return pl.ds(half * PIECE, PIECE)

    def remote(src, owner, kind, half, c0, nc, part, axis, send_idx):
        return pltpu.make_async_remote_copy(
            src_ref=src,
            dst_ref=land.at[owner, kind, rows(half), pl.ds(c0, nc)],
            send_sem=send_sem.at[send_idx],
            recv_sem=recv_sem.at[owner, kind, half, part],
            device_id=(peer(axis),),
            device_id_type=MESH,
        )

    def send(*args):
        started.append(args[5])
        return remote(*args, len(started) - 1)

    for half in range(HALVES):
        for kind in (1, 0):
            for axis in (CORE,) + AXES:
                send(mine[kind].at[rows(half), :], axis, kind, half, 0, WIDTH, 0, axis).start()

    def local_copies(t, owner, half):
        slot = lax.rem(t, 2)
        return [
            pltpu.make_async_copy(land.at[owner, kind, rows(half), :], bufs.at[slot, kind], buf_sem.at[slot, kind])
            for kind in (0, 1)
        ]

    def arrive(p):
        owner, half = ORDER[p]
        for kind in (1, 0):
            for c0, nc, part in PARTS[owner]:
                view = land.at[owner, kind, rows(half), pl.ds(c0, nc)]
                remote(view, owner, kind, half, c0, nc, part, CORE, 0).wait_recv()
        for copy in local_copies(p, owner, half):
            copy.start()
        if owner % 2 == 0:
            for kind in (1, 0):
                whole = land.at[owner, kind, rows(half), :]
                send(whole, owner ^ CORE, kind, half, 0, WIDTH, 0, CORE).start()
                for axis, c0, nc, part in FORWARD.get(owner, []):
                    view = land.at[owner, kind, rows(half), pl.ds(c0, nc)]
                    send(view, owner ^ axis, kind, half, c0, nc, part, axis).start()

    t2 = par[0]
    b2 = par[1]

    def work(texts, images, row_off=None):
        sy = dot_t(xo[...], texts)
        sx = dot_t(yo[...], images)
        hy = text_weights(sy, t2, b2, stats, row_off)
        au[...] += dot_n(hy, texts)
        hx = image_weights(sx, t2, b2, row_off)
        av[...] += dot_n(hx, images)

    for c in own_copies:
        c.wait()

    def own_step(half, carry):
        off = pl.multiple_of(half * PIECE, PIECE)
        work(yo[pl.ds(off, PIECE), :], xo[pl.ds(off, PIECE), :], off)
        return carry

    lax.fori_loop(0, HALVES, own_step, 0)
    arrive(0)

    def at_step(t, lo, hi):
        if hi - lo == 1:
            arrive(lo + 1)
            return
        mid = (lo + hi) // 2

        @pl.when(t < mid)
        def _():
            at_step(t, lo, mid)

        @pl.when(t >= mid)
        def _():
            at_step(t, mid, hi)

    total = len(ORDER)

    def step(t, carry):
        for copy in local_copies(t, 1, 0):
            copy.wait()

        @pl.when(t < total - 1)
        def _():
            at_step(t, 0, total - 1)

        slot = lax.rem(t, 2)
        work(bufs[slot, 1], bufs[slot, 0])
        return carry

    lax.fori_loop(0, total, step, 0)
    for idx, cols in enumerate(started):
        view = land.at[1, 0, rows(0), pl.ds(0, cols)]
        remote(view, 1, 0, 0, 0, cols, 0, CORE, idx).wait_send()


N_SENDS = 2 * HALVES * (4 + 7 + sum(len(v) for v in FORWARD.values()))


def solution(mesh):
    group_size = mesh.shape["dp"]

    def local_fn(img_emb, txt_emb, log_temp, logit_bias):
        total_rows = ROWS * group_size
        img_unit, img_inv = normalize_rows(img_emb)
        txt_unit, txt_inv = normalize_rows(txt_emb)
        img_b = img_unit.astype(jnp.bfloat16)
        txt_b = txt_unit.astype(jnp.bfloat16)
        temp_scale = jnp.exp(log_temp)
        par = jnp.stack([temp_scale * LOG2E, logit_bias * LOG2E])
        hbm = pl.BlockSpec(memory_space=pl.ANY)
        vmem = pl.BlockSpec(memory_space=pltpu.VMEM)
        acc_shape = jax.ShapeDtypeStruct((ROWS, WIDTH), jnp.float32)
        au, av, stats, _ = pl.pallas_call(
            kernel,
            out_shape=(
                acc_shape,
                acc_shape,
                jax.ShapeDtypeStruct((4, 8, PIECE), jnp.float32),
                jax.ShapeDtypeStruct((16, 2, ROWS, WIDTH), jnp.bfloat16),
            ),
            in_specs=[pl.BlockSpec(memory_space=pltpu.SMEM), hbm, hbm],
            out_specs=(vmem, vmem, vmem, hbm),
            scratch_shapes=[
                pltpu.VMEM((ROWS, WIDTH), jnp.bfloat16),
                pltpu.VMEM((ROWS, WIDTH), jnp.bfloat16),
                pltpu.VMEM((2, 2, PIECE, WIDTH), jnp.bfloat16),
                pltpu.SemaphoreType.DMA((2,)),
                pltpu.SemaphoreType.DMA((2, 2)),
                pltpu.SemaphoreType.DMA((N_SENDS,)),
                pltpu.SemaphoreType.DMA((16, 2, HALVES, 3)),
            ],
            compiler_params=pltpu.CompilerParams(
                collective_id=0, has_side_effects=True, vmem_limit_bytes=60 * 2**20
            ),
        )(par, img_b, txt_b)
        sums = jnp.sum(stats, axis=(1, 2))
        local = jnp.stack([LN2 * sums[0] + sums[3], sums[1], sums[2]])
        total = lax.psum(local, "dp") / total_rows
        grad_img = project_back(img_unit, img_inv, temp_scale * au)
        grad_txt = project_back(txt_unit, txt_inv, temp_scale * av)
        return total[0], grad_img, grad_txt, temp_scale * total[2], total[1]

    return jax.shard_map(
        local_fn,
        mesh=mesh,
        in_specs=(P("dp", None), P("dp", None), P(), P()),
        out_specs=(P(), P("dp", None), P("dp", None), P(), P()),
        check_vma=False,
    )
```

time: 1440 us -> 342 us (0.24)
  waiting for transfers between devices: 977 us -> 0 us
  matrix products: 299 us -> 0 us
  Pallas kernels: 0 us -> 280 us
  blocking collectives: 78.1 us -> 32 us
  other arithmetic: 54.5 us -> 22.3 us
  local copies, waits for them, and re-layouts: 23.1 us -> 2.54 us
    ppermute x31 -> x0, waiting for transfers between devices: 977 us -> none  [the longest x15 530 us: visit_step(): txt_acc = lax.ppermute(txt_acc, 'dp', shift_pairs)]
    dot_general x48 -> x0, matrix products: 299 us -> none  [the longest x16 126 us: pair_terms(): jnp.einsum('id,jd->ij', img_b, txt_blk, preferred_element_type=jnp.float32)]
    pallas_call x0 -> x1, Pallas kernels: none -> 280 us  [local_fn(): pl.pallas_call(kernel, out_shape=(acc_shape, acc_shape, jax.ShapeDtypeStr...]
    psum x1, blocking collectives: 78.1 us -> 32 us  [local_fn(): total = lax.psum(local, 'dp') / total_rows]
    add x15 -> x0, other arithmetic: 30.7 us -> none  [visit_step(): stat_sums + new_sums]
    while x135 -> x0, local copies, waits for them, and re-layouts: 22.2 us -> none
  transfers between devices with their start and end apart: 31 -> 0, of which waited for: 30 -> 0; matrix products, arithmetic and copies ran while one was open for 16% -> 0% of each run, Pallas kernels for 0% -> 0%
where the time goes in v1:
time: 342 us
  Pallas kernels  280 us (82%)
  blocking collectives  32 us (9%)
  other arithmetic  22.3 us (7%)
  between operations  5.28 us (2%)
    pallas_call x1, Pallas kernels, local_fn(): pl.pallas_call(kernel, out_shape=(acc_shape, acc_shape, jax.ShapeDtypeStr...  280 us
    psum x1, blocking collectives, local_fn(): total = lax.psum(local, 'dp') / total_rows  32 us

profile of v1, /device:TPU:0, one launch (start us, length us, event | category | flops | bytes accessed | tf_op | source)
XLA Modules:
  0.0 341.8 jit_solution(5857798072377558581)
XLA Ops:
  0.6 0.0 copy-start
  2.1 0.6 pad_maximum_fusion.par
  2.7 0.0 copy-start.1
  2.7 2.3 fusion.9
  5.1 2.2 fusion.13
  7.3 0.0 copy-done
  7.3 1.9 fusion.2.yb
  9.2 0.0 copy-done.1
  9.2 1.9 fusion.5.xb
  11.0 279.6 %shard_map.83 = (f32[1024,1152]{1,0:T(8,128)}, f32[1024,1152]{1,0:T(8,128)}, f32[4,8,512]{2,1,0:T(8,128)}, bf16[16,2,1024,1152]{3,2,1,0:T(8,128)(2,1)}) custom-call(f32[2]{0:T(128)} %pad_maximum_fusion.par, bf16[1024,1152]{1,0:T(8,128)(2,1)} %fusion.5.xb, bf16[1024,1152]{1,0:T(8,128)(2,1)} %fusion.2.yb), custom_call_target="tpu_custom_call" | custom-call | tf_op jit(solution)/shard_map/pallas_call | solution.py:263
  290.7 1.0 reduce_sum.47
  291.6 0.1 slice.22
  291.7 0.6 fusion.15
  293.6 0.1 pad_maximum_fusion.1
  293.6 32.0 %psum.7 = f32[3]{0:T(128)S(1)} all-reduce(f32[3]{0:T(128)S(1)} %pad_maximum_fusion.1), channel_id=1, replica_groups=mesh['dp'=16] {'dp'}, use_global_device_ids=true, to_apply=%region_3.0 | all-reduce | flops 3 | bytes 24 | tf_op jit(solution)/shard_map/psum | solution.py:288
  325.7 0.6 fusion.14
  326.9 0.0 copy-start.4
  326.9 5.8 %fusion.6 = (f32[1024]{0:T(1024)S(1)}, f32[1024]{0:T(1024)S(1)}) fusion(bf16[1024,1152]{1,0:T(8,128)(2,1)} %param.4, f32[1024,1152]{1,0:T(8,128)} %get-tuple-element.9, f32[]{:T(128)S(6)} %exp.3, f32[1024]{0:T(1024)S(1)} %rsqrt.16, f32[1024,1152]{1,0:T(8,128)} %get-tuple-element.10, f32[1024]{0:T(1024)S(1)} %rsqrt.17, bf16[1024,1152]{1,0:T(8,128)(2,1)S(1)} %copy-done), kind=kLoop, calls=%fused_computation.10 | loop fusion | flops 11794432 | bytes 14172164 | tf_op jit(solution)/shard_map/reduce_sum | solution.py:52
  332.7 0.0 copy-done.4
  332.8 0.0 copy-start.2
  332.8 0.0 copy-start.3
  332.8 3.5 %fusion.12 = f32[1024,1152]{1,0:T(8,128)} fusion(bf16[1024,1152]{1,0:T(8,128)(2,1)S(1)} %copy-done, f32[1024,1152]{1,0:T(8,128)S(1)} %copy-done.4, f32[1024]{0:T(1024)S(1)} %get-tuple-element.17, f32[]{:T(128)S(6)} %exp.3, f32[1024]{0:T(1024)S(1)} %rsqrt.17), kind=kLoop, calls=%fused_computation.16 | loop fusion | flops 7077888 | bytes 11804676 | tf_op jit(solution)/shard_map/mul | solution.py:53
  336.3 0.0 copy-done.2
  336.3 1.3 copy-done.3
  337.5 3.2 fusion.8
  (3 shorter events, 0.0 us)
Async XLA Ops:
  0.6 6.6 %copy-start = (bf16[1024,1152]{1,0:T(8,128)(2,1)S(1)}, bf16[1024,1152]{1,0:T(8,128)(2,1)}, u32[]{:S(2)}) copy-start(bf16[1024,1152]{1,0:T(8,128)(2,1)} %param.5) | copy-start | bytes 7077892
  2.7 6.4 %copy-start.1 = (bf16[1024,1152]{1,0:T(8,128)(2,1)S(1)}, bf16[1024,1152]{1,0:T(8,128)(2,1)}, u32[]{:S(2)}) copy-start(bf16[1024,1152]{1,0:T(8,128)(2,1)} %param.4) | copy-start | bytes 7077892
  326.9 5.8 %copy-start.4 = (f32[1024,1152]{1,0:T(8,128)S(1)}, f32[1024,1152]{1,0:T(8,128)}, u32[]{:S(2)}) copy-start(f32[1024,1152]{1,0:T(8,128)} %get-tuple-element.10) | copy-start | bytes 14155780
  332.8 3.5 %copy-start.2 = (bf16[1024,1152]{1,0:T(8,128)(2,1)S(1)}, bf16[1024,1152]{1,0:T(8,128)(2,1)}, u32[]{:S(2)}) copy-start(bf16[1024,1152]{1,0:T(8,128)(2,1)} %param.4) | copy-start | bytes 7077892
  332.8 4.8 %copy-start.3 = (f32[1024,1152]{1,0:T(8,128)S(1)}, f32[1024,1152]{1,0:T(8,128)}, u32[]{:S(2)}) copy-start(f32[1024,1152]{1,0:T(8,128)} %get-tuple-element.9) | copy-start | bytes 14155780

commit v2 on v1

v2 whole, which is shorter than its diff:
```python
import jax
import jax.numpy as jnp
from jax import lax
from jax.experimental import pallas as pl
from jax.experimental.pallas import tpu as pltpu
from jax.sharding import PartitionSpec as P

LOG2E = 1.4426950408889634
LN2 = 0.6931471805599453
MESH = pl.DeviceIdType.MESH
ROWS = 1024
WIDTH = 1152
PIECE = 256
QUARTERS = ROWS // PIECE
CORE, AX, AY, AZ = 1, 2, 4, 8
AXES = (AX, AY, AZ)

FORWARD = {
    2: [(AY, 384, 768, 0), (AZ, 384, 384, 0)],
    4: [(AZ, 0, 768, 0), (AX, 0, 384, 1)],
    8: [(AX, 0, 384, 1), (AX, 768, 384, 2), (AY, 768, 384, 1)],
    6: [(AZ, 384, 384, 0)],
    12: [(AX, 0, 384, 1)],
    10: [(AY, 768, 384, 2)],
}
PARTS = {m: [(0, WIDTH, 0)] for m in (1, 2, 4, 8, 3, 5, 9, 7, 13, 11, 15)}
for _m, _sends in FORWARD.items():
    for _axis, _c0, _nc, _part in _sends:
        PARTS.setdefault(_m ^ _axis, []).append((_c0, _nc, _part))

_FAR = (6, 12, 10)
EVEN = [(m, q) for q in range(4) for m in AXES]
EVEN += [(m, q) for q in range(4) for m in _FAR]
EVEN += [(14, q) for q in range(4)]
_odd = [(m ^ CORE, q) for m, q in EVEN]
STEPS = [((1, 0), (1, 1)), (EVEN[0], (1, 2))]
STEPS += [(EVEN[k], _odd[k - 1]) for k in range(1, 27)]
STEPS += [(_odd[26], (1, 3)), (EVEN[27], _odd[27])]


def dot_t(a, b):
    return lax.dot_general(a, b, (((1,), (1,)), ((), ())), preferred_element_type=jnp.float32)


def dot_n(a, b):
    return lax.dot_general(a, b, (((1,), (0,)), ((), ())), preferred_element_type=jnp.float32)


def fold8(v):
    rows, cols = v.shape
    return jnp.sum(v.reshape(rows // 8, 8, cols), axis=0)


def text_weights(s, t2, b2, stats, row_off=None):
    rows, cols = s.shape
    step = 64
    out = []
    acc = [None, None, None]
    prod = None
    for r in range(0, rows, step):
        sc = s[r : r + step]
        logit = sc * t2 + b2
        small = jnp.exp2(-jnp.abs(logit))
        recip = 1.0 / (1.0 + small)
        other = small * recip
        pos = logit >= 0
        h = jnp.where(pos, recip, other)
        over = jnp.maximum(logit, 0.0)
        if row_off is not None:
            ri = lax.broadcasted_iota(jnp.int32, sc.shape, 0) + r
            ci = lax.broadcasted_iota(jnp.int32, sc.shape, 1) + row_off
            own = ri == ci
            h = jnp.where(own, -jnp.where(pos, other, recip), h)
            over = jnp.where(own, over - logit, over)
        sums = [fold8(over), fold8(h), fold8(h * sc)]
        acc = [b if a is None else a + b for a, b in zip(acc, sums)]
        q = small
        while q.shape[0] > 8:
            n = q.shape[0] // 2
            q = q[:n] + q[n:] + q[:n] * q[n:]
        if prod is None:
            prod = q
        elif (r // step) % 8 == 0:
            stats[3] += jnp.log1p(prod)
            prod = q
        else:
            prod = prod + q + prod * q
        out.append(h.astype(jnp.bfloat16))
    stats[3] += jnp.log1p(prod)
    for i in range(3):
        stats[i] += acc[i]
    return jnp.concatenate(out, axis=0)


def image_weights(s, t2, b2, row_off=None):
    logit = s * t2 + b2
    if row_off is None:
        return (1.0 / (1.0 + jnp.exp2(-logit))).astype(jnp.bfloat16)
    ri = lax.broadcasted_iota(jnp.int32, s.shape, 0)
    ci = lax.broadcasted_iota(jnp.int32, s.shape, 1) + row_off
    own = ri == ci
    h = 1.0 / (1.0 + jnp.exp2(jnp.where(own, logit, -logit)))
    return jnp.where(own, -h, h).astype(jnp.bfloat16)


def kernel(
    par, zx, zy, au, av, loss, gtemp, gbias, land, zxv, zyv, xo, yo, bufs, stats,
    own_sem, buf_sem, send_sem, recv_sem, stat_land, stat_send, stat_recv,
):
    me = lax.axis_index("dp")

    def peer(mask):
        at = me
        for bit in (1, 2, 4, 8):
            if mask & bit:
                at = at + bit * (1 - 2 * lax.rem(me // bit, 2))
        return at

    barrier = pltpu.get_barrier_semaphore()
    for mask in range(1, 16):
        pl.semaphore_signal(barrier, inc=1, device_id=(peer(mask),), device_id_type=MESH)

    arrays = ((zx, zxv, xo, au), (zy, zyv, yo, av))

    def rows(q):
        return pl.ds(q * PIECE, PIECE)

    def load(kind, q):
        src, dst = arrays[kind][:2]
        return pltpu.make_async_copy(src.at[rows(q), :], dst.at[rows(q), :], own_sem.at[kind, q])

    def unit_rows(z):
        z32 = z.astype(jnp.float32)
        inv = lax.rsqrt(jnp.sum(z32 * z32, axis=-1, keepdims=True))
        return z32 * inv, inv

    for q in range(QUARTERS):
        for kind in (1, 0):
            load(kind, q).start()
    for q in range(QUARTERS):
        for kind in (1, 0):
            load(kind, q).wait()
            _, raw, unit_b, _ = arrays[kind]
            unit_b[rows(q), :] = unit_rows(raw[rows(q), :])[0].astype(jnp.bfloat16)
    stats[...] = jnp.zeros_like(stats)
    au[...] = jnp.zeros_like(au)
    av[...] = jnp.zeros_like(av)
    pl.semaphore_wait(barrier, 15)

    started = []
    mine = (xo, yo)

    def remote(src, owner, kind, q, c0, nc, part, axis, send_idx):
        return pltpu.make_async_remote_copy(
            src_ref=src,
            dst_ref=land.at[owner, kind, rows(q), pl.ds(c0, nc)],
            send_sem=send_sem.at[send_idx],
            recv_sem=recv_sem.at[owner, kind, q, part],
            device_id=(peer(axis),),
            device_id_type=MESH,
        )

    def send(*args):
        started.append(args[5])
        return remote(*args, len(started) - 1)

    for q in range(QUARTERS):
        for kind in (1, 0):
            for axis in (CORE,) + AXES:
                send(mine[kind].at[rows(q), :], axis, kind, q, 0, WIDTH, 0, axis).start()

    def local_copy(t, owner, q, kind, chunk):
        slot = lax.rem(t, 2)
        return pltpu.make_async_copy(
            land.at[owner, kind, rows(q), :], bufs.at[slot, kind, rows(chunk), :], buf_sem.at[slot, kind, chunk]
        )

    def arrive(p):
        for chunk, (owner, q) in enumerate(STEPS[p]):
            for kind in (1, 0):
                for c0, nc, part in PARTS[owner]:
                    view = land.at[owner, kind, rows(q), pl.ds(c0, nc)]
                    remote(view, owner, kind, q, c0, nc, part, CORE, 0).wait_recv()
            if owner % 2 == 0:
                for kind in (1, 0):
                    whole = land.at[owner, kind, rows(q), :]
                    send(whole, owner ^ CORE, kind, q, 0, WIDTH, 0, CORE).start()
                    for axis, c0, nc, part in FORWARD.get(owner, []):
                        view = land.at[owner, kind, rows(q), pl.ds(c0, nc)]
                        send(view, owner ^ axis, kind, q, c0, nc, part, axis).start()
            for kind in (1, 0):
                local_copy(p, owner, q, kind, chunk).start()

    t2 = par[0]
    b2 = par[1]

    def work(texts, images, row_off=None):
        sy = dot_t(xo[...], texts)
        sx = dot_t(yo[...], images)
        hy = text_weights(sy, t2, b2, stats, row_off)
        au[...] += dot_n(hy, texts)
        hx = image_weights(sx, t2, b2, row_off)
        av[...] += dot_n(hx, images)

    def own_step(half, carry):
        off = pl.multiple_of(half * 2 * PIECE, 2 * PIECE)
        work(yo[pl.ds(off, 2 * PIECE), :], xo[pl.ds(off, 2 * PIECE), :], off)
        return carry

    lax.fori_loop(0, 2, own_step, 0)
    arrive(0)

    def at_step(t, lo, hi):
        if hi - lo == 1:
            arrive(lo + 1)
            return
        mid = (lo + hi) // 2

        @pl.when(t < mid)
        def _():
            at_step(t, lo, mid)

        @pl.when(t >= mid)
        def _():
            at_step(t, mid, hi)

    last = len(STEPS) - 1

    def step(t, carry):
        @pl.when(t < last - 1)
        def _():
            at_step(t, 0, last - 1)

        @pl.when(t == last)
        def _():
            arrive(last)

        for kind in (1, 0):
            for chunk in (0, 1):
                local_copy(t, 1, 0, kind, chunk).wait()
        slot = lax.rem(t, 2)
        work(bufs[slot, 1], bufs[slot, 0])
        return carry

    lax.fori_loop(0, last + 1, step, 0)

    acc = stats[...]
    stat_land[0] = acc[:, :, 0:128] + acc[:, :, 128:256] + acc[:, :, 256:384] + acc[:, :, 384:512]

    def stat_copy(mask):
        return pltpu.make_async_remote_copy(
            src_ref=stat_land.at[0],
            dst_ref=stat_land.at[mask],
            send_sem=stat_send.at[mask],
            recv_sem=stat_recv.at[mask],
            device_id=(peer(mask),),
            device_id_type=MESH,
        )

    for mask in range(15, 0, -1):
        stat_copy(mask).start()

    def project(i, carry):
        at = pl.ds(pl.multiple_of(i * 128, 128), 128)
        for _, raw, _, acc in arrays:
            unit, inv = unit_rows(raw[at, :])
            grad = par[2] * acc[at, :]
            radial = jnp.sum(unit * grad, axis=-1, keepdims=True)
            acc[at, :] = (grad - unit * radial) * inv
        return carry

    lax.fori_loop(0, ROWS // 128, project, 0)
    for idx, cols in enumerate(started):
        view = land.at[1, 0, rows(0), pl.ds(0, cols)]
        remote(view, 1, 0, 0, 0, cols, 0, CORE, idx).wait_send()
    for mask in range(1, 16):
        stat_copy(mask).wait()
    tree = [stat_land[m] for m in range(16)]
    while len(tree) > 1:
        tree = [tree[i] + tree[i + 1] for i in range(0, len(tree), 2)]
    total = tree[0]
    inv_rows = 1.0 / (ROWS * 16)
    loss[0] = (LN2 * jnp.sum(total[0]) + jnp.sum(total[3])) * inv_rows
    gbias[0] = jnp.sum(total[1]) * inv_rows
    gtemp[0] = par[2] * (jnp.sum(total[2]) * inv_rows)


N_SENDS = 2 * QUARTERS * (4 + 7 + sum(len(v) for v in FORWARD.values()))


def solution(mesh):
    def local_fn(img_emb, txt_emb, log_temp, logit_bias):
        temp_scale = jnp.exp(log_temp)
        par = jnp.stack([temp_scale * LOG2E, logit_bias * LOG2E, temp_scale])
        hbm = pl.BlockSpec(memory_space=pl.ANY)
        vmem = pl.BlockSpec(memory_space=pltpu.VMEM)
        smem = pl.BlockSpec(memory_space=pltpu.SMEM)
        acc_shape = jax.ShapeDtypeStruct((ROWS, WIDTH), jnp.float32)
        one = jax.ShapeDtypeStruct((1,), jnp.float32)
        whole = pltpu.VMEM((ROWS, WIDTH), jnp.bfloat16)
        gx, gy, loss, gtemp, gbias, _ = pl.pallas_call(
            kernel,
            out_shape=(
                acc_shape,
                acc_shape,
                one,
                one,
                one,
                jax.ShapeDtypeStruct((16, 2, ROWS, WIDTH), jnp.bfloat16),
            ),
            in_specs=[smem, hbm, hbm],
            out_specs=(vmem, vmem, smem, smem, smem, hbm),
            scratch_shapes=[
                whole,
                whole,
                whole,
                whole,
                pltpu.VMEM((2, 2, 2 * PIECE, WIDTH), jnp.bfloat16),
                pltpu.VMEM((4, 8, 2 * PIECE), jnp.float32),
                pltpu.SemaphoreType.DMA((2, QUARTERS)),
                pltpu.SemaphoreType.DMA((2, 2, 2)),
                pltpu.SemaphoreType.DMA((N_SENDS,)),
                pltpu.SemaphoreType.DMA((16, 2, QUARTERS, 3)),
                pltpu.VMEM((16, 4, 8, 128), jnp.float32),
                pltpu.SemaphoreType.DMA((16,)),
                pltpu.SemaphoreType.DMA((16,)),
            ],
            compiler_params=pltpu.CompilerParams(
                collective_id=0, has_side_effects=True, vmem_limit_bytes=62 * 2**20
            ),
        )(par, img_emb, txt_emb)
        return loss[0], gx, gy, gtemp[0], gbias[0]

    return jax.shard_map(
        local_fn,
        mesh=mesh,
        in_specs=(P("dp", None), P("dp", None), P(), P()),
        out_specs=(P(), P("dp", None), P("dp", None), P(), P()),
        check_vma=False,
    )
```

time: 342 us -> 295 us (0.86)
  blocking collectives: 32 us -> 0 us
  other arithmetic: 22.3 us -> 0.59 us
  local copies, waits for them, and re-layouts: 2.54 us -> 7.17 us
    psum x1 -> x0, blocking collectives: 32 us -> none  [local_fn(): total = lax.psum(local, 'dp') / total_rows]
    reduce_sum x4 -> x0, other arithmetic: 11.3 us -> none  [the longest x1 5.8 us: project_back(): radial = jnp.sum(unit_rows * grad_dir, axis=-1, keepdims=True)]
    mul x2 -> x0, other arithmetic: 6.65 us -> none  [project_back(): return (grad_dir - unit_rows * radial) * inv_norm]
    unnamed x10 -> x4, local copies, waits for them, and re-layouts: 1.28 us -> 7.17 us
    convert_element_type x2 -> x0, other arithmetic: 3.73 us -> none  [the longest x1 1.86 us: local_fn(): txt_b = txt_unit.astype(jnp.bfloat16)]
where the time goes in v2:
time: 295 us
  Pallas kernels  280 us (95%)
  local copies, waits for them, and re-layouts  7.17 us (2%)
  between operations  7.15 us (2%)
    pallas_call x1, Pallas kernels, local_fn(): pl.pallas_call(kernel, out_shape=(acc_shape, acc_shape, one, one, one, ja...  280 us
    unnamed x4, local copies, waits for them, and re-layouts  7.17 us

profile of v2, /device:TPU:0, one launch (start us, length us, event | category | flops | bytes accessed | tf_op | source)
XLA Modules:
  0.0 294.9 jit_solution(14659396058638463606)
XLA Ops:
  2.0 0.6 pad_maximum_fusion.par
  2.6 280.0 %shard_map.83 = (f32[1024,1152]{1,0:T(8,128)}, f32[1024,1152]{1,0:T(8,128)}, f32[1]{0:T(128)}, f32[1]{0:T(128)}, f32[1]{0:T(128)}, /*index=5*/bf16[16,2,1024,1152]{3,2,1,0:T(8,128)(2,1)}) custom-call(f32[3]{0:T(128)} %pad_maximum_fusion.par, bf16[1024,1152]{1,0:T(8,128)(2,1)} %zx.1, bf16[1024,1152]{1,0:T(8,128)(2,1)} %zy.1), custom_call_target="tpu_custom_call" | custom-call | tf_op jit(solution)/shard_map/pallas_call | solution.py:301
  283.1 0.0 copy-start
  283.2 5.0 %copy.17 = f32[1024,1152]{1,0:T(8,128)} copy(f32[1024,1152]{1,0:T(8,128)} %get-tuple-element.21) | data formatting | bytes 9437184
  288.1 0.0 copy-done
  288.1 2.2 copy.18
Async XLA Ops:
  283.1 5.0 %copy-start = (f32[1024,1152]{1,0:T(8,128)S(1)}, f32[1024,1152]{1,0:T(8,128)}, u32[]{:S(2)}) copy-start(f32[1024,1152]{1,0:T(8,128)} %get-tuple-element.22) | copy-start | bytes 14155780

commit v3 on v2

v3 whole, which is shorter than its diff:
```python
import jax
import jax.numpy as jnp
from jax import lax
from jax.experimental import pallas as pl
from jax.experimental.pallas import tpu as pltpu
from jax.sharding import PartitionSpec as P

LOG2E = 1.4426950408889634
LN2 = 0.6931471805599453
MESH = pl.DeviceIdType.MESH
ROWS = 1024
WIDTH = 1152
PIECE = 256
LAG = 1
DIRECT = 20
QUARTERS = ROWS // PIECE
CORE, AX, AY, AZ = 1, 2, 4, 8
AXES = (AX, AY, AZ)

FORWARD = {
    2: [(AY, 384, 768, 0), (AZ, 384, 384, 0)],
    4: [(AZ, 0, 768, 0), (AX, 0, 384, 1)],
    8: [(AX, 0, 384, 1), (AX, 768, 384, 2), (AY, 768, 384, 1)],
    6: [(AZ, 384, 384, 0)],
    12: [(AX, 0, 384, 1)],
    10: [(AY, 768, 384, 2)],
}
PARTS = {m: [(0, WIDTH, 0)] for m in (1, 2, 4, 8, 3, 5, 9, 7, 13, 11, 15)}
for _m, _sends in FORWARD.items():
    for _axis, _c0, _nc, _part in _sends:
        PARTS.setdefault(_m ^ _axis, []).append((_c0, _nc, _part))

_FAR = (6, 12, 10)
EVEN = [(m, q) for q in range(4) for m in AXES]
EVEN += [(m, q) for q in range(4) for m in _FAR]
EVEN += [(14, q) for q in range(4)]
_odd = [(m ^ CORE, q) for m, q in EVEN]
STEPS = [((1, 0), (1, 1)), (EVEN[0], (1, 2))]
STEPS += [(EVEN[k], _odd[k - 1]) for k in range(1, 27)]
STEPS += [(_odd[26], (1, 3)), (EVEN[27], _odd[27])]


SPOT = {}
for _p in range(DIRECT, len(STEPS)):
    for _chunk, _piece in enumerate(STEPS[_p]):
        if _piece[0] != 1:
            SPOT[_piece] = (_p - DIRECT + 2, _chunk)


def is_late(p):
    if p >= DIRECT:
        return True
    return any(piece in EVEN and EVEN.index(piece) % 3 == 0 for piece in STEPS[p])


def dot_t(a, b):
    return lax.dot_general(a, b, (((1,), (1,)), ((), ())), preferred_element_type=jnp.float32)


def dot_n(a, b):
    return lax.dot_general(a, b, (((1,), (0,)), ((), ())), preferred_element_type=jnp.float32)


def fold8(v):
    rows, cols = v.shape
    return jnp.sum(v.reshape(rows // 8, 8, cols), axis=0)


def text_weights(s, t2, b2, stats, row_off=None):
    rows, cols = s.shape
    step = 64
    out = []
    acc = [None, None, None]
    prod = None
    for r in range(0, rows, step):
        sc = s[r : r + step]
        logit = sc * t2 + b2
        small = jnp.exp2(-jnp.abs(logit))
        recip = 1.0 / (1.0 + small)
        other = small * recip
        pos = logit >= 0
        h = jnp.where(pos, recip, other)
        over = jnp.maximum(logit, 0.0)
        if row_off is not None:
            ri = lax.broadcasted_iota(jnp.int32, sc.shape, 0) + r
            ci = lax.broadcasted_iota(jnp.int32, sc.shape, 1) + row_off
            own = ri == ci
            h = jnp.where(own, -jnp.where(pos, other, recip), h)
            over = jnp.where(own, over - logit, over)
        sums = [fold8(over), fold8(h), fold8(h * sc)]
        acc = [b if a is None else a + b for a, b in zip(acc, sums)]
        q = small
        while q.shape[0] > 8:
            n = q.shape[0] // 2
            q = q[:n] + q[n:] + q[:n] * q[n:]
        if prod is None:
            prod = q
        elif (r // step) % 8 == 0:
            stats[3] += jnp.log1p(prod)
            prod = q
        else:
            prod = prod + q + prod * q
        out.append(h.astype(jnp.bfloat16))
    stats[3] += jnp.log1p(prod)
    for i in range(3):
        stats[i] += acc[i]
    return jnp.concatenate(out, axis=0)


def image_weights(s, t2, b2, row_off=None):
    logit = s * t2 + b2
    if row_off is None:
        return (1.0 / (1.0 + jnp.exp2(-logit))).astype(jnp.bfloat16)
    ri = lax.broadcasted_iota(jnp.int32, s.shape, 0)
    ci = lax.broadcasted_iota(jnp.int32, s.shape, 1) + row_off
    own = ri == ci
    h = 1.0 / (1.0 + jnp.exp2(jnp.where(own, logit, -logit)))
    return jnp.where(own, -h, h).astype(jnp.bfloat16)


def unit_rows(z):
    z32 = z.astype(jnp.float32)
    inv = lax.rsqrt(jnp.sum(z32 * z32, axis=-1, keepdims=True))
    return z32 * inv, inv


def project_kernel(par, stats, zx, zy, au, av, gx, gy, loss, gtemp, gbias):
    for src, acc, dst in ((zx, au, gx), (zy, av, gy)):
        unit, inv = unit_rows(src[...])
        grad = par[2] * acc[...]
        radial = jnp.sum(unit * grad, axis=-1, keepdims=True)
        dst[...] = (grad - unit * radial) * inv

    @pl.when(pl.program_id(0) == 0)
    def _():
        inv_rows = 1.0 / (ROWS * 16)
        loss[0] = (LN2 * jnp.sum(stats[0]) + jnp.sum(stats[3])) * inv_rows
        gbias[0] = jnp.sum(stats[1]) * inv_rows
        gtemp[0] = par[2] * (jnp.sum(stats[2]) * inv_rows)


def kernel(
    par, zx, zy, out_u, out_v, total, land, xo, yo, au, av, bufs, stats,
    own_sem, buf_sem, out_sem, send_sem, recv_sem, stat_land, stat_send, stat_recv,
):
    me = lax.axis_index("dp")

    def peer(mask):
        at = me
        for bit in (1, 2, 4, 8):
            if mask & bit:
                at = at + bit * (1 - 2 * lax.rem(me // bit, 2))
        return at

    barrier = pltpu.get_barrier_semaphore()
    for mask in range(1, 16):
        pl.semaphore_signal(barrier, inc=1, device_id=(peer(mask),), device_id_type=MESH)

    arrays = ((zx, xo), (zy, yo))

    def rows(q):
        return pl.ds(q * PIECE, PIECE)

    def load(kind, q):
        src, dst = arrays[kind]
        return pltpu.make_async_copy(src.at[rows(q), :], dst.at[rows(q), :], own_sem.at[kind, q])

    for q in range(QUARTERS):
        for kind in (1, 0):
            load(kind, q).start()

    started = []
    mine = (xo, yo)

    def place(owner, kind, q, c0, nc):
        if (owner, q) in SPOT:
            slot, chunk = SPOT[owner, q]
            return bufs.at[slot, kind, rows(chunk), pl.ds(c0, nc)]
        return land.at[owner, kind, rows(q), pl.ds(c0, nc)]

    def remote(src, owner, kind, q, c0, nc, part, axis, send_idx):
        return pltpu.make_async_remote_copy(
            src_ref=src,
            dst_ref=place(owner, kind, q, c0, nc),
            send_sem=send_sem.at[send_idx],
            recv_sem=recv_sem.at[owner, kind, q, part],
            device_id=(peer(axis),),
            device_id_type=MESH,
        )

    def send(*args):
        started.append(args[5])
        return remote(*args, len(started) - 1)

    for q in range(QUARTERS):
        for kind in (1, 0):
            load(kind, q).wait()
            emb = arrays[kind][1]
            emb[rows(q), :] = unit_rows(emb[rows(q), :])[0].astype(jnp.bfloat16)
        if q == 0:
            pl.semaphore_wait(barrier, 15)
        for kind in (1, 0):
            for axis in (CORE,) + AXES:
                send(mine[kind].at[rows(q), :], axis, kind, q, 0, WIDTH, 0, axis).start()
    stats[...] = jnp.zeros_like(stats)
    au[...] = jnp.zeros_like(au)
    av[...] = jnp.zeros_like(av)

    def local_copy(p, owner, q, kind, chunk):
        return pltpu.make_async_copy(
            land.at[owner, kind, rows(q), :],
            bufs.at[slot_of(p), kind, rows(chunk), :],
            buf_sem.at[lax.rem(p, 2), kind, chunk],
        )

    def arrive(p, kind):
        for chunk, (owner, q) in enumerate(STEPS[p]):
            for c0, nc, part in PARTS[owner]:
                view = place(owner, kind, q, c0, nc)
                remote(view, owner, kind, q, c0, nc, part, CORE, 0).wait_recv()
            if owner % 2 == 0:
                whole = place(owner, kind, q, 0, WIDTH)
                send(whole, owner ^ CORE, kind, q, 0, WIDTH, 0, CORE).start()
                for axis, c0, nc, part in FORWARD.get(owner, []):
                    view = place(owner, kind, q, c0, nc)
                    send(view, owner ^ axis, kind, q, c0, nc, part, axis).start()
        for chunk, (owner, q) in enumerate(STEPS[p]):
            if (owner, q) not in SPOT:
                local_copy(p, owner, q, kind, chunk).start()
                if p >= DIRECT:
                    local_copy(p, owner, q, kind, chunk).wait()

    def slot_of(p):
        far = p // DIRECT
        return lax.rem(p, 2) * (1 - far) + (p - DIRECT + 2) * far

    def ready(p, kind):
        @pl.when(p < DIRECT)
        def _():
            for chunk in (0, 1):
                local_copy(p, 1, 0, kind, chunk).wait()

    last = len(STEPS) - 1
    t2 = par[0]
    b2 = par[1]

    def own_step(half, carry):
        off = pl.multiple_of(half * 2 * PIECE, 2 * PIECE)
        texts = yo[pl.ds(off, 2 * PIECE), :]
        images = xo[pl.ds(off, 2 * PIECE), :]
        sy = dot_t(xo[...], texts)
        sx = dot_t(yo[...], images)
        au[...] += dot_n(text_weights(sy, t2, b2, stats, off), texts)
        av[...] += dot_n(image_weights(sx, t2, b2, off), images)
        return carry

    def events(t, todo, lo, hi):
        if not any(todo.get(i) for i in range(lo, hi)):
            return
        if hi - lo == 1:
            for p, kind in todo[lo]:
                arrive(p, kind)
            return
        mid = (lo + hi) // 2

        @pl.when(t < mid)
        def _():
            events(t, todo, lo, mid)

        @pl.when(t >= mid)
        def _():
            events(t, todo, mid, hi)

    def phase(count, wanted, body):
        early = {t: [i for i in wanted(t) if not is_late(i[0])] for t in range(count)}
        late = {t: [i for i in wanted(t) if is_late(i[0])] for t in range(count)}

        def one(t, carry):
            events(t, early, 0, count)
            body(t)
            events(t, late, 0, count)
            return carry

        lax.fori_loop(0, count, one, 0)

    lax.fori_loop(0, 2, own_step, 0)
    arrive(0, 1)

    def text_step(t):
        ready(t, 1)
        texts = bufs[slot_of(t), 1]
        au[...] += dot_n(text_weights(dot_t(xo[...], texts), t2, b2, stats), texts)

    phase(LAG, lambda t: [(t + 1, 1)] + ([(0, 0)] if t == LAG - 1 else []), text_step)

    def pair_step(t):
        ready(t + LAG, 1)
        ready(t, 0)
        texts = bufs[slot_of(t + LAG), 1]
        images = bufs[slot_of(t), 0]
        sy = dot_t(xo[...], texts)
        sx = dot_t(yo[...], images)
        au[...] += dot_n(text_weights(sy, t2, b2, stats), texts)
        av[...] += dot_n(image_weights(sx, t2, b2), images)

    pairs = len(STEPS) - LAG
    phase(
        pairs,
        lambda t: ([(t + LAG + 1, 1)] if t + LAG < last else []) + ([(t + 1, 0)] if t + 1 < pairs else []),
        pair_step,
    )

    acc = stats[...]
    stat_land[0] = acc[:, :, 0:128] + acc[:, :, 128:256] + acc[:, :, 256:384] + acc[:, :, 384:512]

    def stat_copy(mask):
        return pltpu.make_async_remote_copy(
            src_ref=stat_land.at[0],
            dst_ref=stat_land.at[mask],
            send_sem=stat_send.at[mask],
            recv_sem=stat_recv.at[mask],
            device_id=(peer(mask),),
            device_id_type=MESH,
        )

    for mask in range(15, 0, -1):
        stat_copy(mask).start()
    flush_u = pltpu.make_async_copy(au, out_u, out_sem.at[0])
    flush_u.start()

    arrive(last, 0)
    images = bufs[slot_of(last), 0]
    av[...] += dot_n(image_weights(dot_t(yo[...], images), t2, b2), images)
    flush_v = pltpu.make_async_copy(av, out_v, out_sem.at[1])
    flush_v.start()
    for idx, cols in enumerate(started):
        view = land.at[1, 0, rows(0), pl.ds(0, cols)]
        remote(view, 1, 0, 0, 0, cols, 0, CORE, idx).wait_send()
    for mask in range(1, 16):
        stat_copy(mask).wait()
    tree = [stat_land[m] for m in range(16)]
    while len(tree) > 1:
        tree = [tree[i] + tree[i + 1] for i in range(0, len(tree), 2)]
    total[...] = tree[0]
    flush_u.wait()
    flush_v.wait()


N_SENDS = 2 * QUARTERS * (4 + 7 + sum(len(v) for v in FORWARD.values()))


def solution(mesh):
    def local_fn(img_emb, txt_emb, log_temp, logit_bias):
        temp_scale = jnp.exp(log_temp)
        par = jnp.stack([temp_scale * LOG2E, logit_bias * LOG2E, temp_scale])
        hbm = pl.BlockSpec(memory_space=pl.ANY)
        vmem = pl.BlockSpec(memory_space=pltpu.VMEM)
        smem = pl.BlockSpec(memory_space=pltpu.SMEM)
        block = pl.BlockSpec((256, WIDTH), lambda i: (i, 0))
        acc_shape = jax.ShapeDtypeStruct((ROWS, WIDTH), jnp.float32)
        one = jax.ShapeDtypeStruct((1,), jnp.float32)
        emb = pltpu.VMEM((ROWS, WIDTH), jnp.bfloat16)
        acc = pltpu.VMEM((ROWS, WIDTH), jnp.float32)
        au, av, stats, _ = pl.pallas_call(
            kernel,
            out_shape=(
                acc_shape,
                acc_shape,
                jax.ShapeDtypeStruct((4, 8, 128), jnp.float32),
                jax.ShapeDtypeStruct((16, 2, ROWS, WIDTH), jnp.bfloat16),
            ),
            in_specs=[smem, hbm, hbm],
            out_specs=(hbm, hbm, vmem, hbm),
            scratch_shapes=[
                emb,
                emb,
                acc,
                acc,
                pltpu.VMEM((2 + len(STEPS) - DIRECT, 2, 2 * PIECE, WIDTH), jnp.bfloat16),
                pltpu.VMEM((4, 8, 2 * PIECE), jnp.float32),
                pltpu.SemaphoreType.DMA((2, QUARTERS)),
                pltpu.SemaphoreType.DMA((2, 2, 2)),
                pltpu.SemaphoreType.DMA((2,)),
                pltpu.SemaphoreType.DMA((N_SENDS,)),
                pltpu.SemaphoreType.DMA((16, 2, QUARTERS, 3)),
                pltpu.VMEM((16, 4, 8, 128), jnp.float32),
                pltpu.SemaphoreType.DMA((16,)),
                pltpu.SemaphoreType.DMA((16,)),
            ],
            compiler_params=pltpu.CompilerParams(
                collective_id=0, has_side_effects=True, vmem_limit_bytes=62 * 2**20
            ),
        )(par, img_emb, txt_emb)
        gx, gy, loss, gtemp, gbias = pl.pallas_call(
            project_kernel,
            grid=(ROWS // 256,),
            out_shape=(acc_shape, acc_shape, one, one, one),
            in_specs=[smem, pl.BlockSpec((4, 8, 128), lambda i: (0, 0, 0)), block, block, block, block],
            out_specs=(block, block, smem, smem, smem),
        )(par, stats, img_emb, txt_emb, au, av)
        return loss[0], gx, gy, gtemp[0], gbias[0]

    return jax.shard_map(
        local_fn,
        mesh=mesh,
        in_specs=(P("dp", None), P("dp", None), P(), P()),
        out_specs=(P(), P("dp", None), P("dp", None), P(), P()),
        check_vma=False,
    )
```

time: 295 us -> 281 us (0.953)
  local copies, waits for them, and re-layouts: 7.17 us -> 0 us
  between operations: 7.15 us -> 2.09 us
    unnamed x4 -> x0, local copies, waits for them, and re-layouts: 7.17 us -> none
    pallas_call x1 -> x2, Pallas kernels: 280 us -> 278 us  [the longest x1 268 us: local_fn(): pl.pallas_call(kernel, out_shape=(acc_shape, acc_shape, jax.ShapeDtypeStr...]
where the time goes in v3:
time: 281 us
  Pallas kernels  278 us (99%)
    pallas_call x1, Pallas kernels, local_fn(): pl.pallas_call(kernel, out_shape=(acc_shape, acc_shape, jax.ShapeDtypeStr...  268 us
    pallas_call x1, Pallas kernels, local_fn(): pl.pallas_call(project_kernel, grid=(ROWS // 256,), out_shape=(acc_shape,...  10.3 us

profile of v3, /device:TPU:0, one launch (start us, length us, event | category | flops | bytes accessed | tf_op | source)
XLA Modules:
  0.0 280.8 jit_solution(3772276354403201487)
XLA Ops:
  2.0 0.6 pad_maximum_fusion.par
  2.6 267.8 %shard_map.83 = (f32[1024,1152]{1,0:T(8,128)}, f32[1024,1152]{1,0:T(8,128)}, f32[4,8,128]{2,1,0:T(8,128)}, bf16[16,2,1024,1152]{3,2,1,0:T(8,128)(2,1)}) custom-call(f32[3]{0:T(128)} %pad_maximum_fusion.par, bf16[1024,1152]{1,0:T(8,128)(2,1)} %zx.3, bf16[1024,1152]{1,0:T(8,128)(2,1)} %zy.3), custom_call_target="tpu_custom_call" | custom-call | tf_op jit(solution)/shard_map/pallas_call | solution.py:364
  270.4 10.3 %shard_map.84 = (f32[1024,1152]{1,0:T(8,128)}, f32[1024,1152]{1,0:T(8,128)}, f32[1]{0:T(128)}, f32[1]{0:T(128)}, f32[1]{0:T(128)}) custom-call(f32[3]{0:T(128)} %pad_maximum_fusion.par, f32[4,8,128]{2,1,0:T(8,128)} %get-tuple-element.13.stats, bf16[1024,1152]{1,0:T(8,128)(2,1)} %zx.3, bf16[1024,1152]{1,0:T(8,128)(2,1)} %zy.3, ...), custom_call_target="tpu_custom_call" | custom-call | tf_op jit(solution)/shard_map/pallas_call | solution.py:394

commit v4 on v3

--- a/solution.py
+++ b/solution.py
@@ -35,16 +35,14 @@
 EVEN += [(m, q) for q in range(4) for m in _FAR]
 EVEN += [(14, q) for q in range(4)]
 _odd = [(m ^ CORE, q) for m, q in EVEN]
-STEPS = [((1, 0), (1, 1)), (EVEN[0], (1, 2))]
-STEPS += [(EVEN[k], _odd[k - 1]) for k in range(1, 27)]
-STEPS += [(_odd[26], (1, 3)), (EVEN[27], _odd[27])]
-
+STEPS = [((1, 0), (1, 1)), ((1, 2), (1, 3)), (EVEN[0], EVEN[1]), (EVEN[2], _odd[0])]
+STEPS += [(EVEN[k], _odd[k - 2]) for k in range(3, 28)]
+STEPS += [(_odd[26], _odd[27])]
 
 SPOT = {}
 for _p in range(DIRECT, len(STEPS)):
     for _chunk, _piece in enumerate(STEPS[_p]):
-        if _piece[0] != 1:
-            SPOT[_piece] = (_p - DIRECT + 2, _chunk)
+        SPOT[_piece] = (_p - DIRECT + 2, _chunk)
 
 
 def is_late(p):
@@ -124,10 +122,11 @@
     return z32 * inv, inv
 
 
-def project_kernel(par, stats, zx, zy, au, av, gx, gy, loss, gtemp, gbias):
+def project_kernel(stats, zx, zy, au, av, gx, gy, loss, gtemp, gbias):
+    scale = stats[4][0:1, 0:1]
     for src, acc, dst in ((zx, au, gx), (zy, av, gy)):
         unit, inv = unit_rows(src[...])
-        grad = par[2] * acc[...]
+        grad = scale * acc[...]
         radial = jnp.sum(unit * grad, axis=-1, keepdims=True)
         dst[...] = (grad - unit * radial) * inv
 
@@ -136,11 +135,11 @@
         inv_rows = 1.0 / (ROWS * 16)
         loss[0] = (LN2 * jnp.sum(stats[0]) + jnp.sum(stats[3])) * inv_rows
         gbias[0] = jnp.sum(stats[1]) * inv_rows
-        gtemp[0] = par[2] * (jnp.sum(stats[2]) * inv_rows)
+        gtemp[0] = jnp.max(stats[4]) * (jnp.sum(stats[2]) * inv_rows)
 
 
 def kernel(
-    par, zx, zy, out_u, out_v, total, land, xo, yo, au, av, bufs, stats,
+    log_temp, logit_bias, zx, zy, out_u, out_v, total, land, xo, yo, au, av, bufs, stats,
     own_sem, buf_sem, out_sem, send_sem, recv_sem, stat_land, stat_send, stat_recv,
 ):
     me = lax.axis_index("dp")
@@ -225,10 +224,8 @@
                     view = place(owner, kind, q, c0, nc)
                     send(view, owner ^ axis, kind, q, c0, nc, part, axis).start()
         for chunk, (owner, q) in enumerate(STEPS[p]):
-            if (owner, q) not in SPOT:
+            if p < DIRECT:
                 local_copy(p, owner, q, kind, chunk).start()
-                if p >= DIRECT:
-                    local_copy(p, owner, q, kind, chunk).wait()
 
     def slot_of(p):
         far = p // DIRECT
@@ -241,8 +238,9 @@
                 local_copy(p, 1, 0, kind, chunk).wait()
 
     last = len(STEPS) - 1
-    t2 = par[0]
-    b2 = par[1]
+    scale = jnp.exp(jnp.full((8, 128), log_temp[0], jnp.float32))
+    t2 = jnp.max(scale) * LOG2E
+    b2 = logit_bias[0] * LOG2E
 
     def own_step(half, carry):
         off = pl.multiple_of(half * 2 * PIECE, 2 * PIECE)
@@ -341,7 +339,8 @@
     tree = [stat_land[m] for m in range(16)]
     while len(tree) > 1:
         tree = [tree[i] + tree[i + 1] for i in range(0, len(tree), 2)]
-    total[...] = tree[0]
+    total[0:4] = tree[0]
+    total[4] = scale
     flush_u.wait()
     flush_v.wait()
 
@@ -351,12 +350,10 @@
 
 def solution(mesh):
     def local_fn(img_emb, txt_emb, log_temp, logit_bias):
-        temp_scale = jnp.exp(log_temp)
-        par = jnp.stack([temp_scale * LOG2E, logit_bias * LOG2E, temp_scale])
         hbm = pl.BlockSpec(memory_space=pl.ANY)
         vmem = pl.BlockSpec(memory_space=pltpu.VMEM)
         smem = pl.BlockSpec(memory_space=pltpu.SMEM)
-        block = pl.BlockSpec((256, WIDTH), lambda i: (i, 0))
+        block = pl.BlockSpec((512, WIDTH), lambda i: (i, 0))
         acc_shape = jax.ShapeDtypeStruct((ROWS, WIDTH), jnp.float32)
         one = jax.ShapeDtypeStruct((1,), jnp.float32)
         emb = pltpu.VMEM((ROWS, WIDTH), jnp.bfloat16)
@@ -366,10 +363,10 @@
             out_shape=(
                 acc_shape,
                 acc_shape,
-                jax.ShapeDtypeStruct((4, 8, 128), jnp.float32),
+                jax.ShapeDtypeStruct((5, 8, 128), jnp.float32),
                 jax.ShapeDtypeStruct((16, 2, ROWS, WIDTH), jnp.bfloat16),
             ),
-            in_specs=[smem, hbm, hbm],
+            in_specs=[smem, smem, hbm, hbm],
             out_specs=(hbm, hbm, vmem, hbm),
             scratch_shapes=[
                 emb,
@@ -390,14 +387,14 @@
             compiler_params=pltpu.CompilerParams(
                 collective_id=0, has_side_effects=True, vmem_limit_bytes=62 * 2**20
             ),
-        )(par, img_emb, txt_emb)
+        )(log_temp.reshape(1), logit_bias.reshape(1), img_emb, txt_emb)
         gx, gy, loss, gtemp, gbias = pl.pallas_call(
             project_kernel,
-            grid=(ROWS // 256,),
+            grid=(ROWS // 512,),
             out_shape=(acc_shape, acc_shape, one, one, one),
-            in_specs=[smem, pl.BlockSpec((4, 8, 128), lambda i: (0, 0, 0)), block, block, block, block],
+            in_specs=[pl.BlockSpec((5, 8, 128), lambda i: (0, 0, 0)), block, block, block, block],
             out_specs=(block, block, smem, smem, smem),
-        )(par, stats, img_emb, txt_emb, au, av)
+        )(stats, img_emb, txt_emb, au, av)
         return loss[0], gx, gy, gtemp[0], gbias[0]
 
     return jax.shard_map(

time: 281 us -> 275 us (0.979)
  Pallas kernels: 278 us -> 272 us
    pallas_call x1, Pallas kernels: 268 us -> 263 us  [local_fn(): pl.pallas_call(kernel, out_shape=(acc_shape, acc_shape, jax.ShapeDtypeStr...]
where the time goes in v4:
time: 275 us; the launch traced here: 274 us
  Pallas kernels  272 us (99%)
    pallas_call x1, Pallas kernels, local_fn(): pl.pallas_call(kernel, out_shape=(acc_shape, acc_shape, jax.ShapeDtypeStr...  263 us
    pallas_call x1, Pallas kernels, local_fn(): pl.pallas_call(project_kernel, grid=(ROWS // 512,), out_shape=(acc_shape,...  9.25 us

profile of v4, /device:TPU:0, one launch (start us, length us, event | category | flops | bytes accessed | tf_op | source)
XLA Modules:
  0.0 274.4 jit_solution(8600926645470986780)
XLA Ops:
  1.9 263.2 %shard_map.83 = (f32[1024,1152]{1,0:T(8,128)}, f32[1024,1152]{1,0:T(8,128)}, f32[5,8,128]{2,1,0:T(8,128)}, bf16[16,2,1024,1152]{3,2,1,0:T(8,128)(2,1)}) custom-call(f32[1]{0:T(128)} %bitcast.5.log_temp, f32[1]{0:T(128)} %bitcast.6.logit_bias, bf16[1024,1152]{1,0:T(8,128)(2,1)} %zx.3, bf16[1024,1152]{1,0:T(8,128)(2,1)} %zy.3), custom_call_target="tpu_custom_call" | custom-call | tf_op jit(solution)/shard_map/pallas_call | solution.py:361
  265.2 9.2 %shard_map.84 = (f32[1024,1152]{1,0:T(8,128)}, f32[1024,1152]{1,0:T(8,128)}, f32[1]{0:T(128)}, f32[1]{0:T(128)}, f32[1]{0:T(128)}) custom-call(f32[5,8,128]{2,1,0:T(8,128)} %get-tuple-element.13.stats, bf16[1024,1152]{1,0:T(8,128)(2,1)} %zx.3, bf16[1024,1152]{1,0:T(8,128)(2,1)} %zy.3, f32[1024,1152]{1,0:T(8,128)} %get-tuple-element.14.au, ...), custom_call_target="tpu_custom_call" | custom-call | tf_op jit(solution)/shard_map/pallas_call | solution.py:391

commit v5 on v4

--- a/solution.py
+++ b/solution.py
@@ -196,10 +196,9 @@
             load(kind, q).wait()
             emb = arrays[kind][1]
             emb[rows(q), :] = unit_rows(emb[rows(q), :])[0].astype(jnp.bfloat16)
-        if q == 0:
-            pl.semaphore_wait(barrier, 15)
-        for kind in (1, 0):
-            for axis in (CORE,) + AXES:
+            if q == 0 and kind == 1:
+                pl.semaphore_wait(barrier, 15)
+            for axis in AXES + (CORE,):
                 send(mine[kind].at[rows(q), :], axis, kind, q, 0, WIDTH, 0, axis).start()
     stats[...] = jnp.zeros_like(stats)
     au[...] = jnp.zeros_like(au)

time: 275 us -> 275 us (level)
  no operation moved by 1% of the time
where the time goes in v5:
time: 275 us; the launch traced here: 274 us
  Pallas kernels  272 us (99%)
    pallas_call x1, Pallas kernels, local_fn(): pl.pallas_call(kernel, out_shape=(acc_shape, acc_shape, jax.ShapeDtypeStr...  263 us
    pallas_call x1, Pallas kernels, local_fn(): pl.pallas_call(project_kernel, grid=(ROWS // 512,), out_shape=(acc_shape,...  9.25 us

profile of v5, /device:TPU:0, one launch (start us, length us, event | category | flops | bytes accessed | tf_op | source)
XLA Modules:
  0.0 274.4 jit_solution(3346236019749531031)
XLA Ops:
  1.9 263.2 %shard_map.83 = (f32[1024,1152]{1,0:T(8,128)}, f32[1024,1152]{1,0:T(8,128)}, f32[5,8,128]{2,1,0:T(8,128)}, bf16[16,2,1024,1152]{3,2,1,0:T(8,128)(2,1)}) custom-call(f32[1]{0:T(128)} %bitcast.5.log_temp, f32[1]{0:T(128)} %bitcast.6.logit_bias, bf16[1024,1152]{1,0:T(8,128)(2,1)} %zx.3, bf16[1024,1152]{1,0:T(8,128)(2,1)} %zy.3), custom_call_target="tpu_custom_call" | custom-call | tf_op jit(solution)/shard_map/pallas_call | solution.py:360
  265.1 9.2 %shard_map.84 = (f32[1024,1152]{1,0:T(8,128)}, f32[1024,1152]{1,0:T(8,128)}, f32[1]{0:T(128)}, f32[1]{0:T(128)}, f32[1]{0:T(128)}) custom-call(f32[5,8,128]{2,1,0:T(8,128)} %get-tuple-element.13.stats, bf16[1024,1152]{1,0:T(8,128)(2,1)} %zx.3, bf16[1024,1152]{1,0:T(8,128)(2,1)} %zy.3, f32[1024,1152]{1,0:T(8,128)} %get-tuple-element.14.au, ...), custom_call_target="tpu_custom_call" | custom-call | tf_op jit(solution)/shard_map/pallas_call | solution.py:390
